TPU v7x, 32 devices: a whole 2x2x4 slice. The times are simulated.
32 devices in a mesh: seq: 16 (over z, y, core), sub: 2 (over x).
Axes of the slice: x: 2, y: 2, z: 4, core: 2. Of those that a mesh axis runs over, the one named last changes fastest.
Arguments:
- tokens: bfloat16 [4096, 1024], P(('seq', 'sub')), may hold values from -6 to 6
- cotangent: bfloat16 [4096, 1024], P(('seq', 'sub')), may hold values from -6 to 6
- fine_qkv: bfloat16 [1024, 3, 1024], replicated, may hold values from -0.1875 to 0.1875
- fine_out: bfloat16 [1024, 1024], replicated, may hold values from -0.1875 to 0.1875
- coarse_qkv: bfloat16 [1024, 3, 1024], P(None, None, 'sub'), may hold values from -0.1875 to 0.1875
- coarse_out: bfloat16 [1024, 1024], P('sub'), may hold values from -0.5 to 0.5
Outputs:
- output: bfloat16 [4096, 1024], P(('seq', 'sub'))
- grad_tokens: bfloat16 [4096, 1024], P(('seq', 'sub'))
All inputs are finite; a program needn't handle non-finite values.
Results may differ from a plain program's by a relative error of at most 0.02.
Values may be sent and summed in bfloat16 or wider, within the bound.
A program may use at most 128 MiB of HBM per device.

v0:
```python
import jax
import jax.numpy as jnp
from jax import lax
from jax.sharding import PartitionSpec as P

D = 1024
HEADS = 16
HEAD_DIM = 64
WINDOW = 512
POOL = 16


EPS = 1e-06


def from_behind(value, axis, steps):
    count = lax.axis_size(axis)
    first, last = (max(0, -steps), min(count, count - steps))
    return lax.ppermute(value, axis, [(source, source + steps) for source in range(first, last)])


def rms_rows(values):
    widened = values.astype(jnp.float32)
    factor = lax.rsqrt(jnp.mean(widened * widened, axis=-1, keepdims=True) + EPS)
    return (widened * factor, factor)


def norm_back(grad_rows, normed, factor):
    return factor * (grad_rows - normed * jnp.mean(normed * grad_rows, axis=-1, keepdims=True))


def project_rows(normed_b, weight):
    row_count = normed_b.shape[0]
    local_width = weight.shape[2]
    projected = jnp.dot(
        normed_b,
        weight.reshape(weight.shape[0], 3 * local_width),
        preferred_element_type=jnp.float32,
    )
    projected = projected.reshape(row_count, 3, local_width // HEAD_DIM, HEAD_DIM)
    query_unit, query_scale = rms_rows(projected[:, 0])
    key_unit, key_scale = rms_rows(projected[:, 1])
    return (query_unit, query_scale, key_unit, key_scale, projected[:, 2])


def contract_last(left, right):
    return lax.dot_general(
        left, right, (((1,), (1,)), ((), ())), preferred_element_type=jnp.float32
    )


def window_exp(query_blk, key_blk, first_pos):
    scores = jnp.einsum(
        "qhd,khd->hqk", query_blk, key_blk, preferred_element_type=jnp.float32
    ) * HEAD_DIM ** (-0.5)
    query_pos = lax.broadcasted_iota(jnp.int32, (query_blk.shape[0], key_blk.shape[0]), 0)
    key_pos = lax.broadcasted_iota(jnp.int32, (query_blk.shape[0], key_blk.shape[0]), 1)
    gap = WINDOW + query_pos - key_pos
    allowed = (gap >= 0) & (gap < WINDOW) & (first_pos - WINDOW + key_pos >= 0)
    return jnp.where(allowed[None], jnp.exp(scores), 0.0)


def send_down(rows, distance):
    return from_behind(rows, ("seq", "sub"), distance)


def send_up(rows, distance):
    return from_behind(rows.astype(jnp.bfloat16), ("seq", "sub"), -distance).astype(rows.dtype)


def gather_group(rows):
    return lax.all_gather(rows, "sub", axis=0, tiled=True)


def sum_heads(rows):
    return lax.psum_scatter(
        rows.astype(jnp.bfloat16), "sub", scatter_dimension=0, tiled=True
    ).astype(jnp.float32)


def per_device(tokens, cotangent, fine_qkv, fine_out, coarse_qkv, coarse_out):
    row_count = tokens.shape[0]
    score_scale = HEAD_DIM ** (-0.5)
    lead_rows = POOL - 1
    tail_rows = min(WINDOW, row_count)
    hop_count = -(-WINDOW // row_count)
    margin = hop_count * tail_rows
    block_rows = min(row_count, 512)
    anchor = lax.axis_index(("seq", "sub")) * row_count
    normed_fine, scale_fine = rms_rows(tokens)
    query_unit1, query_scale1, key_unit1, key_scale1, value_raw1 = project_rows(
        normed_fine.astype(jnp.bfloat16), fine_qkv
    )
    query_one = query_unit1.astype(jnp.bfloat16)
    key_one = key_unit1.astype(jnp.bfloat16)
    value_one = value_raw1.astype(jnp.bfloat16)
    own_tail = jnp.stack([key_one.reshape(tail_rows, D), value_one.reshape(tail_rows, D)])
    earlier = []
    for distance in range(1, hop_count + 1):
        earlier.append(send_down(own_tail, distance))
    key_all = jnp.concatenate(
        [pieces[0] for pieces in earlier[::-1]] + [key_one.reshape(row_count, D)]
    ).reshape(margin + row_count, HEADS, HEAD_DIM)
    value_all = jnp.concatenate(
        [pieces[1] for pieces in earlier[::-1]] + [value_one.reshape(row_count, D)]
    ).reshape(margin + row_count, HEADS, HEAD_DIM)
    block_start = 0
    numer = window_exp(query_one, key_all, anchor + block_start)
    totals = jnp.sum(numer, axis=-1)
    probs_half = (numer / totals[:, :, None]).astype(jnp.bfloat16)
    attended_list = jnp.einsum(
        "hqk,khd->qhd", probs_half, value_all, preferred_element_type=jnp.float32
    ).astype(jnp.bfloat16)
    hidden = (
        tokens.astype(jnp.float32)
        + jnp.dot(attended_list.reshape(row_count, D), fine_out, preferred_element_type=jnp.float32)
    ).astype(jnp.bfloat16)
    carried_rows = send_down(hidden[row_count - lead_rows :], 1)
    shifted = jnp.concatenate([carried_rows, hidden[: row_count - lead_rows]])
    pooled = (
        shifted.reshape(row_count // POOL, POOL, D)
        .astype(jnp.float32)
        .mean(axis=1)
        .astype(jnp.bfloat16)
    )
    group_in = gather_group(pooled)
    group_size = group_in.shape[0]
    local_width = coarse_qkv.shape[2]
    local_heads = local_width // HEAD_DIM
    normed_coarse, scale_coarse = rms_rows(group_in)
    query_unit2, query_scale2, key_unit2, key_scale2, value_raw2 = project_rows(
        normed_coarse.astype(jnp.bfloat16), coarse_qkv
    )
    query_two = query_unit2.astype(jnp.bfloat16)
    key_two = key_unit2.astype(jnp.bfloat16)
    value_two = value_raw2.astype(jnp.bfloat16)
    every_key, every_value = (
        lax.all_gather(key_two.reshape(group_size, local_width), "seq", axis=0, tiled=True),
        lax.all_gather(value_two.reshape(group_size, local_width), "seq", axis=0, tiled=True),
    )
    coarse_len = every_key.shape[0]
    every_key = every_key.reshape(coarse_len, local_heads, HEAD_DIM)
    every_value = every_value.reshape(coarse_len, local_heads, HEAD_DIM)
    group_start = lax.axis_index("seq") * group_size
    query_pos = group_start + lax.broadcasted_iota(jnp.int32, (group_size, coarse_len), 0)
    key_pos = lax.broadcasted_iota(jnp.int32, (group_size, coarse_len), 1)
    scores_two = (
        jnp.einsum("qhd,khd->hqk", query_two, every_key, preferred_element_type=jnp.float32)
        * score_scale
    )
    numer_two = jnp.where((key_pos <= query_pos)[None], jnp.exp(scores_two), 0.0)
    totals_two = jnp.sum(numer_two, axis=-1)
    probs_full2 = numer_two / totals_two[:, :, None]
    probs_half2 = probs_full2.astype(jnp.bfloat16)
    attended_two = jnp.einsum(
        "hqk,khd->qhd", probs_half2, every_value, preferred_element_type=jnp.float32
    ).astype(jnp.bfloat16)
    mixed_rows = sum_heads(
        jnp.dot(
            attended_two.reshape(group_size, local_width),
            coarse_out,
            preferred_element_type=jnp.float32,
        )
    )
    coarse_state = (pooled.astype(jnp.float32) + mixed_rows).astype(jnp.bfloat16)
    output = (
        hidden.astype(jnp.float32) + jnp.repeat(coarse_state, POOL, axis=0).astype(jnp.float32)
    ).astype(jnp.bfloat16)
    grad_rows = cotangent.astype(jnp.float32)
    coarse_grad = grad_rows.reshape(row_count // POOL, POOL, D).sum(axis=1)
    group_grad = gather_group(coarse_grad.astype(jnp.bfloat16))
    grad_att2 = (
        contract_last(group_grad, coarse_out)
        .astype(jnp.bfloat16)
        .reshape(group_size, local_heads, HEAD_DIM)
    )
    deltas_two = jnp.sum(grad_att2.astype(jnp.float32) * attended_two.astype(jnp.float32), axis=-1)
    prob_grad2 = jnp.einsum(
        "qhd,khd->hqk", grad_att2, every_value, preferred_element_type=jnp.float32
    )
    dscore_two = (probs_full2 * (prob_grad2 - deltas_two.T[:, :, None])).astype(jnp.bfloat16)
    query_grad2 = (
        jnp.einsum("hqk,khd->qhd", dscore_two, every_key, preferred_element_type=jnp.float32)
        * score_scale
    )
    key_terms = jnp.concatenate(
        [
            (
                jnp.einsum(
                    "hqk,qhd->khd", dscore_two, query_two, preferred_element_type=jnp.float32
                )
                * score_scale
            ).reshape(coarse_len, local_width),
            jnp.einsum(
                "hqk,qhd->khd", probs_half2, grad_att2, preferred_element_type=jnp.float32
            ).reshape(coarse_len, local_width),
        ],
        axis=1,
    )
    summed = lax.psum_scatter(
        key_terms.astype(jnp.bfloat16), "seq", scatter_dimension=0, tiled=True
    ).astype(jnp.float32)
    key_grad2 = summed[:, :local_width].reshape(group_size, local_heads, HEAD_DIM)
    value_grad2 = summed[:, local_width:].reshape(group_size, local_heads, HEAD_DIM)
    query_grad2 = norm_back(query_grad2, query_unit2, query_scale2)
    key_grad2 = norm_back(key_grad2, key_unit2, key_scale2)
    qkv_grad2 = (
        jnp.stack([query_grad2, key_grad2, value_grad2], axis=1)
        .astype(jnp.bfloat16)
        .reshape(group_size, 3 * local_width)
    )
    normed_grad2 = sum_heads(contract_last(qkv_grad2, coarse_qkv.reshape(D, 3 * local_width)))
    normed_own, scale_own = rms_rows(pooled)
    pooled_grad = coarse_grad + norm_back(normed_grad2, normed_own, scale_own)
    spread = jnp.repeat(pooled_grad / POOL, POOL, axis=0)
    incoming = send_up(spread[:lead_rows], 1)
    hidden_grad = grad_rows + jnp.concatenate([spread[lead_rows:], incoming])
    grad_att1 = (
        contract_last(hidden_grad.astype(jnp.bfloat16), fine_out)
        .astype(jnp.bfloat16)
        .reshape(row_count, HEADS, HEAD_DIM)
    )
    deltas_one = jnp.sum(grad_att1.astype(jnp.float32) * attended_list.astype(jnp.float32), axis=-1)
    key_grad_all = jnp.zeros((margin + row_count, HEADS, HEAD_DIM), jnp.float32)
    value_grad_all = jnp.zeros((margin + row_count, HEADS, HEAD_DIM), jnp.float32)
    block_start = 0
    low_key = block_start + margin - WINDOW
    numer = window_exp(query_one, key_all, anchor + block_start)
    probs_full = numer / totals[:, block_start : block_start + block_rows, None]
    prob_grad = jnp.einsum("qhd,khd->hqk", grad_att1, value_all, preferred_element_type=jnp.float32)
    dscore = (probs_full * (prob_grad - deltas_one.T[:, :, None])).astype(jnp.bfloat16)
    query_list = (
        jnp.einsum("hqk,khd->qhd", dscore, key_all, preferred_element_type=jnp.float32)
        * score_scale
    )
    key_grad_all = key_grad_all.at[low_key : low_key + WINDOW + block_rows].add(
        jnp.einsum("hqk,qhd->khd", dscore, query_one, preferred_element_type=jnp.float32)
        * score_scale
    )
    value_grad_all = value_grad_all.at[low_key : low_key + WINDOW + block_rows].add(
        jnp.einsum(
            "hqk,qhd->khd",
            probs_full.astype(jnp.bfloat16),
            grad_att1,
            preferred_element_type=jnp.float32,
        )
    )
    stacked = jnp.stack(
        [key_grad_all.reshape(margin + row_count, D), value_grad_all.reshape(margin + row_count, D)]
    )

    def halo_part(distance):
        return stacked[:, margin - distance * tail_rows : margin - (distance - 1) * tail_rows]

    arriving = send_up(halo_part(1), 1)
    for distance in range(2, hop_count + 1):
        arriving = arriving + send_up(halo_part(distance), distance)
    own_grads = stacked[:, margin:].at[:, row_count - tail_rows :].add(arriving)
    query_grad1 = norm_back(query_list, query_unit1, query_scale1)
    key_grad1 = norm_back(own_grads[0].reshape(row_count, HEADS, HEAD_DIM), key_unit1, key_scale1)
    value_grad1 = own_grads[1].reshape(row_count, HEADS, HEAD_DIM)
    qkv_grad1 = (
        jnp.stack([query_grad1, key_grad1, value_grad1], axis=1)
        .astype(jnp.bfloat16)
        .reshape(row_count, 3 * D)
    )
    normed_grad1 = contract_last(qkv_grad1, fine_qkv.reshape(D, 3 * D))
    grad_tokens = (hidden_grad + norm_back(normed_grad1, normed_fine, scale_fine)).astype(
        jnp.bfloat16
    )
    return (output, grad_tokens)


def solution(mesh):
    placed = (
        P(("seq", "sub"), None),
        P(("seq", "sub"), None),
        P(),
        P(),
        P(None, None, "sub"),
        P("sub", None),
    )
    return jax.shard_map(
        per_device,
        mesh=mesh,
        in_specs=placed,
        out_specs=(P(("seq", "sub"), None), P(("seq", "sub"), None)),
        check_vma=False,
    )
```

profile of v0, /device:TPU:5, one launch (start us, length us, event | category | flops | bytes accessed | tf_op | source)
XLA Modules:
  0.0 311.6 jit_solution(8410771166560977054)
XLA Ops:
  8.5 8.7 %copy.9 = bf16[1024,3,1024]{0,2,1:T(8,128)(2,1)} copy(bf16[1024,3,1024]{2,0,1:T(8,128)(2,1)} %param.20) | data formatting | bytes 12582912 | tf_op args[2]
  17.2 4.7 %fusion.43 = f32[128,3,16,64]{0,3,2,1:T(8,128)S(1)} fusion(bf16[3,16,64,1024]{3,2,1,0:T(8,128)(2,1)} %bitcast.177, bf16[128,1024]{1,0:T(8,128)(2,1)S(1)} %copy-done.4, f32[128]{0:T(128)S(1)} %add_rsqrt_fusion.6), kind=kOutput, calls=%fused_computation.81 | convolution fusion | flops 805699584 | bytes 8126976 | tf_op jit(solution)/shard_map/dot_general | solution.py:35
  24.0 3.1 collective-permute-start.3
  27.1 4.0 %collective-permute-start.2 = (bf16[2,128,1024]{1,2,0:T(8,128)(2,1)}, bf16[2,128,1024]{1,2,0:T(8,128)(2,1)}, u32[]{:S(2)}, u32[]{:S(2)}) collective-permute-start(bf16[2,128,1024]{1,2,0:T(8,128)(2,1)} %pad_maximum_fusion.2), channel_id=1, source_target_pairs={{0,2},{1,3},{2,4},{3,5},{4,6},{5,7},{6,8},{7,9},{8,10},{9,11},{10,... | collective-permute-start | bytes 1572872 | tf_op jit(solution)/shard_map/ppermute | solution.py:19
  31.1 3.0 collective-permute-start.1
  34.1 3.1 %collective-permute-start = (bf16[2,128,1024]{1,2,0:T(8,128)(2,1)}, bf16[2,128,1024]{1,2,0:T(8,128)(2,1)}, u32[]{:S(2)}, u32[]{:S(2)}) collective-permute-start(bf16[2,128,1024]{1,2,0:T(8,128)(2,1)} %pad_maximum_fusion.2), channel_id=1, source_target_pairs={{0,4},{1,5},{2,6},{3,7},{4,8},{5,9},{6,10},{7,11},{8,12},{9,13},{1... | collective-permute-start | bytes 1572872 | tf_op jit(solution)/shard_map/ppermute | solution.py:19
  39.2 3.7 %all_gather.15 = bf16[16,1024]{1,0:T(8,128)(2,1)S(1)} all-gather(bf16[8,1024]{1,0:T(8,128)(2,1)S(1)} %convert_element_type.235), channel_id=1, replica_groups=mesh['seq'=16,'sub'=2] {'sub'}, dimensions={0}, use_global_device_ids=true | all-gather | bytes 49152 | tf_op jit(solution)/shard_map/all_gather | solution.py:72
  43.2 13.9 %collective-permute-done.1 = bf16[2,128,1024]{1,2,0:T(8,128)(2,1)} collective-permute-done((bf16[2,128,1024]{1,2,0:T(8,128)(2,1)}, bf16[2,128,1024]{1,2,0:T(8,128)(2,1)}, u32[]{:S(2)}, u32[]{:S(2)}) %collective-permute-start.1) | collective-permute-done | bytes 524320 | tf_op jit(solution)/shard_map/ppermute | solution.py:19
  58.2 6.9 %collective-permute-done = bf16[2,128,1024]{1,2,0:T(8,128)(2,1)} collective-permute-done((bf16[2,128,1024]{1,2,0:T(8,128)(2,1)}, bf16[2,128,1024]{1,2,0:T(8,128)(2,1)}, u32[]{:S(2)}, u32[]{:S(2)}) %collective-permute-start) | collective-permute-done | bytes 524320 | tf_op jit(solution)/shard_map/ppermute | solution.py:19
  74.3 2.1 collective-permute-start.4
  77.8 4.6 %copy.10 = bf16[1024,3,512]{0,2,1:T(8,128)(2,1)} copy(bf16[1024,3,512]{2,0,1:T(8,128)(2,1)} %param.22) | data formatting | bytes 6291456 | tf_op args[4]
  84.2 3.2 %all_gather.12 = bf16[16,1024]{1,0:T(8,128)(2,1)S(1)} all-gather(bf16[8,1024]{1,0:T(8,128)(2,1)S(1)} %get-tuple-element.71), channel_id=1, replica_groups=mesh['seq'=16,'sub'=2] {'sub'}, dimensions={0}, use_global_device_ids=true | all-gather | bytes 49152 | tf_op jit(solution)/shard_map/all_gather | solution.py:72
  87.6 3.2 %fusion.70 = f32[16,3,8,64]{3,0,2,1:T(8,128)S(1)} fusion(bf16[3,8,64,1024]{3,2,1,0:T(8,128)(2,1)} %bitcast.181, bf16[16,1024]{1,0:T(8,128)(2,1)S(1)} %all_gather.12, f32[16]{0:T(128)S(1)} %add_rsqrt_fusion.5), kind=kOutput, calls=%fused_computation.125 | convolution fusion | flops 50380800 | bytes 3276864 | tf_op jit(solution)/shard_map/dot_general | solution.py:35
  96.1 21.3 %all_gather.14 = bf16[256,512]{1,0:T(8,128)(2,1)} all-gather(bf16[16,512]{1,0:T(8,128)(2,1)S(1)} %multiply_convert_fusion.4), channel_id=1, replica_groups=mesh['seq'=16,'sub'=2] {'seq'}, dimensions={0}, use_global_device_ids=true | all-gather | bytes 278528 | tf_op jit(solution)/shard_map/all_gather | solution.py:138
  121.8 23.1 %all_gather.13 = bf16[256,512]{1,0:T(8,128)(2,1)} all-gather(bf16[16,512]{1,0:T(8,128)(2,1)} %convert_element_type.222), channel_id=1, replica_groups=mesh['seq'=16,'sub'=2] {'seq'}, dimensions={0}, use_global_device_ids=true | all-gather | bytes 278528 | tf_op jit(solution)/shard_map/all_gather | solution.py:139
  146.7 2.0 convolution_convert_fusion
  148.8 1.9 multiply_reduce_fusion.5
  163.7 48.0 %reduce-scatter.6.cloned.1.call-done = bf16[16,1024]{1,0:T(8,128)(2,1)} async-done(((bf16[256,1024]{1,0:T(8,128)(2,1)}), bf16[16,1024]{1,0:T(8,128)(2,1)}) %reduce-scatter.6.cloned.1.call-update) | async-done | bytes 32784 | tf_op jit(solution)/shard_map/reduce_scatter | solution.py:200
  216.0 3.1 convolution_convert_fusion.2
  219.8 10.0 %reduce-scatter.8.cloned.1.call-done = bf16[8,1024]{1,0:T(8,128)(2,1)} async-done(((bf16[16,1024]{1,0:T(8,128)(2,1)}), bf16[8,1024]{1,0:T(8,128)(2,1)}) %reduce-scatter.8.cloned.1.call-update) | async-done | bytes 16400 | tf_op jit(solution)/shard_map/reduce_scatter | solution.py:76
  230.8 11.3 %reduce-scatter.4.cloned.1.call-done = bf16[8,1024]{1,0:T(8,128)(2,1)} async-done(((bf16[16,1024]{1,0:T(8,128)(2,1)}), bf16[8,1024]{1,0:T(8,128)(2,1)}) %reduce-scatter.4.cloned.1.call-update) | async-done | bytes 16400 | tf_op jit(solution)/shard_map/reduce_scatter | solution.py:76
  243.0 3.3 %collective-permute-start.5 = (bf16[15,1024]{1,0:T(8,128)(2,1)S(1)}, bf16[15,1024]{1,0:T(8,128)(2,1)S(1)}, u32[]{:S(2)}, u32[]{:S(2)}) collective-permute-start(bf16[15,1024]{1,0:T(8,128)(2,1)S(1)} %slice.258), channel_id=1, source_target_pairs={{1,0},{2,1},{3,2},{4,3},{5,4},{6,5},{7,6},{8,7},{9,8},{10,9},{11,1... | collective-permute-start | bytes 92168 | tf_op jit(solution)/shard_map/ppermute | solution.py:19
  249.7 4.0 %fusion.3 = f32[16,64,640]{2,1,0:T(8,128)S(1)} fusion(bf16[128,16,64]{0,2,1:T(8,128)(2,1)S(1)} %bitcast.194, f32[16,128,640]{2,1,0:T(8,128)} %copy-done.23, f32[16,128]{1,0:T(8,128)S(1)} %copy-done.25, pred[128,640]{1,0:T(8,128)(4,1)} %fusion.39), kind=kOutput, calls=%fused_computation.9 | convolution fusion | flops 173015040 | bytes 8216576 | tf_op jit(solution)/shard_map/hqk,qhd->khd/dot_general | solution.py:241
  253.7 3.8 %multiply_convert_fusion = bf16[16,128,640]{2,1,0:T(8,128)(2,1)S(1)} fusion(f32[16,128]{1,0:T(8,128)S(1)} %bitcast.211, bf16[128,16,64]{0,2,1:T(8,128)(2,1)S(1)} %bitcast.195, bf16[640,16,64]{0,2,1:T(8,128)(2,1)S(1)} %copy-done.19, f32[16,128]{1,0:T(8,128)S(1)} %copy-done.25, f32[16,128,640]{2,1,0:T(8,128)} %copy-done.23, pred[128,640]{1,0:T(8,128)(4,1)S(1)} %copy-done.17), kind=kOutput, calls=%fused_computation.4 | convolution fusion | flops 175636480 | bytes 9535488 | tf_op jit(solution)/shard_map/qhd,khd->hqk/dot_general | solution.py:230
  259.0 4.3 %collective-permute-start.6 = (bf16[2,128,1024]{1,2,0:T(8,128)(2,1)S(1)}, bf16[2,128,1024]{1,2,0:T(8,128)(2,1)S(1)}, u32[]{:S(2)}, u32[]{:S(2)}) collective-permute-start(bf16[2,128,1024]{1,2,0:T(8,128)(2,1)S(1)} %get-tuple-element.72), channel_id=1, source_target_pairs={{1,0},{2,1},{3,2},{4,3},{5,4},{6,5},{7,6},{8,7},{9,8},{10,9},{11,1... | collective-permute-start | bytes 1572872 | tf_op jit(solution)/shard_map/ppermute | solution.py:19
  263.3 1.9 collective-permute-start.9
  265.2 1.9 collective-permute-start.8
  267.1 3.4 %collective-permute-start.7 = (bf16[2,128,1024]{1,2,0:T(8,128)(2,1)S(1)}, bf16[2,128,1024]{1,2,0:T(8,128)(2,1)S(1)}, u32[]{:S(2)}, u32[]{:S(2)}) collective-permute-start(bf16[2,128,1024]{1,2,0:T(8,128)(2,1)S(1)} %get-tuple-element.75), channel_id=1, source_target_pairs={{2,0},{3,1},{4,2},{5,3},{6,4},{7,5},{8,6},{9,7},{10,8},{11,9},{12,... | collective-permute-start | bytes 1572872 | tf_op jit(solution)/shard_map/ppermute | solution.py:19
  272.5 2.0 collective-permute-done.6
  274.5 5.6 %collective-permute-done.9 = bf16[2,128,1024]{1,2,0:T(8,128)(2,1)S(1)} collective-permute-done((bf16[2,128,1024]{1,2,0:T(8,128)(2,1)S(1)}, bf16[2,128,1024]{1,2,0:T(8,128)(2,1)S(1)}, u32[]{:S(2)}, u32[]{:S(2)}) %collective-permute-start.9) | collective-permute-done | bytes 524320 | tf_op jit(solution)/shard_map/ppermute | solution.py:19
  280.0 13.7 %collective-permute-done.8 = bf16[2,128,1024]{1,2,0:T(8,128)(2,1)S(1)} collective-permute-done((bf16[2,128,1024]{1,2,0:T(8,128)(2,1)S(1)}, bf16[2,128,1024]{1,2,0:T(8,128)(2,1)S(1)}, u32[]{:S(2)}, u32[]{:S(2)}) %collective-permute-start.8) | collective-permute-done | bytes 524320 | tf_op jit(solution)/shard_map/ppermute | solution.py:19
  293.7 8.0 %collective-permute-done.7 = bf16[2,128,1024]{1,2,0:T(8,128)(2,1)S(1)} collective-permute-done((bf16[2,128,1024]{1,2,0:T(8,128)(2,1)S(1)}, bf16[2,128,1024]{1,2,0:T(8,128)(2,1)S(1)}, u32[]{:S(2)}, u32[]{:S(2)}) %collective-permute-start.7) | collective-permute-done | bytes 524320 | tf_op jit(solution)/shard_map/ppermute | solution.py:19
  (173 shorter events, 60.0 us)
Async XLA Ops:
  7.2 65.9 %copy-start = (bf16[1024,1024]{1,0:T(8,128)(2,1)S(1)}, bf16[1024,1024]{1,0:T(8,128)(2,1)}, u32[]{:S(2)}) copy-start(bf16[1024,1024]{1,0:T(8,128)(2,1)} %param.21) | copy-start | bytes 6291460
  7.2 204.5 %reduce-scatter.6.cloned.1.call-start = ((), (), s32[]{:S(2)}) async-start(), calls=%async_computation.4 | async-start | bytes 557056 | tf_op jit(solution)/shard_map/reduce_scatter | solution.py:200
  8.5 8.7 %copy-start.20 = (f32[128]{0:T(128)}, f32[128]{0:T(128)S(1)}, u32[]{:S(2)}) copy-start(f32[128]{0:T(128)S(1)} %add_rsqrt_fusion.6) | copy-start | bytes 1540
  8.5 8.7 %copy-start.4 = (bf16[128,1024]{1,0:T(8,128)(2,1)S(1)}, bf16[128,1024]{1,0:T(8,128)(2,1)}, u32[]{:S(2)}) copy-start(bf16[128,1024]{1,0:T(8,128)(2,1)} %param.18) | copy-start | bytes 786436
  21.9 20.9 %copy-start.5 = (bf16[512,1024]{1,0:T(8,128)(2,1)S(1)}, bf16[512,1024]{1,0:T(8,128)(2,1)}, u32[]{:S(2)}) copy-start(bf16[512,1024]{1,0:T(8,128)(2,1)} %param.23) | copy-start | bytes 3145732
  24.0 43.4 %collective-permute-start.3 = (bf16[2,128,1024]{1,2,0:T(8,128)(2,1)}, bf16[2,128,1024]{1,2,0:T(8,128)(2,1)}, u32[]{:S(2)}, u32[]{:S(2)}) collective-permute-start(bf16[2,128,1024]{1,2,0:T(8,128)(2,1)} %pad_maximum_fusion.2), channel_id=1, source_target_pairs={{0,1},{1,2},{2,3},{3,4},{4,5},{5,6},{6,7},{7,8},{8,9},{9,10},{10,1... | collective-permute-start | bytes 1572872 | tf_op jit(solution)/shard_map/ppermute | solution.py:19
  27.1 39.1 %collective-permute-start.2 = (bf16[2,128,1024]{1,2,0:T(8,128)(2,1)}, bf16[2,128,1024]{1,2,0:T(8,128)(2,1)}, u32[]{:S(2)}, u32[]{:S(2)}) collective-permute-start(bf16[2,128,1024]{1,2,0:T(8,128)(2,1)} %pad_maximum_fusion.2), channel_id=1, source_target_pairs={{0,2},{1,3},{2,4},{3,5},{4,6},{5,7},{6,8},{7,9},{8,10},{9,11},{10,... | collective-permute-start | bytes 1572872 | tf_op jit(solution)/shard_map/ppermute | solution.py:19
  31.1 26.0 %collective-permute-start.1 = (bf16[2,128,1024]{1,2,0:T(8,128)(2,1)}, bf16[2,128,1024]{1,2,0:T(8,128)(2,1)}, u32[]{:S(2)}, u32[]{:S(2)}) collective-permute-start(bf16[2,128,1024]{1,2,0:T(8,128)(2,1)} %pad_maximum_fusion.2), channel_id=1, source_target_pairs={{0,3},{1,4},{2,5},{3,6},{4,7},{5,8},{6,9},{7,10},{8,11},{9,12},{10... | collective-permute-start | bytes 1572872 | tf_op jit(solution)/shard_map/ppermute | solution.py:19
  34.1 31.0 %collective-permute-start = (bf16[2,128,1024]{1,2,0:T(8,128)(2,1)}, bf16[2,128,1024]{1,2,0:T(8,128)(2,1)}, u32[]{:S(2)}, u32[]{:S(2)}) collective-permute-start(bf16[2,128,1024]{1,2,0:T(8,128)(2,1)} %pad_maximum_fusion.2), channel_id=1, source_target_pairs={{0,4},{1,5},{2,6},{3,7},{4,8},{5,9},{6,10},{7,11},{8,12},{9,13},{1... | collective-permute-start | bytes 1572872 | tf_op jit(solution)/shard_map/ppermute | solution.py:19
  58.2 10.4 %copy-start.2 = (f32[128,3,16,64]{0,3,2,1:T(8,128)S(1)}, f32[128,3,16,64]{0,3,2,1:T(8,128)}, u32[]{:S(2)}) copy-start(f32[128,3,16,64]{0,3,2,1:T(8,128)} %copy-done.1) | copy-start | bytes 4718596
  68.7 2.0 copy-start.18
  70.7 2.4 copy-start.23
  70.7 2.4 copy-start.24
  74.3 9.1 %collective-permute-start.4 = (bf16[15,1024]{1,0:T(8,128)(2,1)S(1)}, bf16[15,1024]{1,0:T(8,128)(2,1)S(1)}, u32[]{:S(2)}, u32[]{:S(2)}) collective-permute-start(bf16[15,1024]{1,0:T(8,128)(2,1)S(1)} %slice.188), channel_id=1, source_target_pairs={{0,1},{1,2},{2,3},{3,4},{4,5},{5,6},{6,7},{7,8},{8,9},{9,10},{10,1... | collective-permute-start | bytes 92168 | tf_op jit(solution)/shard_map/ppermute | solution.py:19
  95.3 53.5 %copy-start.15 = (bf16[16,8,64]{2,1,0:T(8,128)(2,1)S(1)}, bf16[16,8,64]{2,1,0:T(8,128)(2,1)}, u32[]{:S(2)}) copy-start(bf16[16,8,64]{2,1,0:T(8,128)(2,1)} %reshape.388) | copy-start | bytes 49156
  159.2 70.7 %reduce-scatter.8.cloned.1.call-start = ((), (), s32[]{:S(2)}) async-start(), calls=%async_computation.5 | async-start | bytes 49152 | tf_op jit(solution)/shard_map/reduce_scatter | solution.py:76
  163.7 55.7 %copy-start.22 = (f32[8]{0:T(128)S(1)}, f32[8]{0:T(128)}, u32[]{:S(2)}) copy-start(f32[8]{0:T(128)} %get-tuple-element.70) | copy-start | bytes 100
  216.0 31.6 %copy-start.9 = (bf16[128,1024]{1,0:T(8,128)(2,1)S(1)}, bf16[128,1024]{1,0:T(8,128)(2,1)}, u32[]{:S(2)}) copy-start(bf16[128,1024]{1,0:T(8,128)(2,1)} %param.19) | copy-start | bytes 786436
  219.1 23.0 %reduce-scatter.4.cloned.1.call-start = ((), (), s32[]{:S(2)}) async-start(), calls=%async_computation.3 | async-start | bytes 49152 | tf_op jit(solution)/shard_map/reduce_scatter | solution.py:76
  243.0 6.7 %copy-start.25 = (f32[16,128]{1,0:T(8,128)S(1)}, f32[16,128]{1,0:T(8,128)}, u32[]{:S(2)}) copy-start(f32[16,128]{1,0:T(8,128)} %copy-done.24) | copy-start | bytes 24580
  243.0 4.7 %collective-permute-start.5 = (bf16[15,1024]{1,0:T(8,128)(2,1)S(1)}, bf16[15,1024]{1,0:T(8,128)(2,1)S(1)}, u32[]{:S(2)}, u32[]{:S(2)}) collective-permute-start(bf16[15,1024]{1,0:T(8,128)(2,1)S(1)} %slice.258), channel_id=1, source_target_pairs={{1,0},{2,1},{3,2},{4,3},{5,4},{6,5},{7,6},{8,7},{9,8},{10,9},{11,1... | collective-permute-start | bytes 92168 | tf_op jit(solution)/shard_map/ppermute | solution.py:19
  249.7 4.0 %copy-start.17 = (pred[128,640]{1,0:T(8,128)(4,1)S(1)}, pred[128,640]{1,0:T(8,128)(4,1)}, u32[]{:S(2)}) copy-start(pred[128,640]{1,0:T(8,128)(4,1)} %fusion.39) | copy-start | bytes 245764
  249.7 4.0 %copy-start.19 = (bf16[640,16,64]{0,2,1:T(8,128)(2,1)S(1)}, bf16[640,16,64]{0,2,1:T(8,128)(2,1)}, u32[]{:S(2)}) copy-start(bf16[640,16,64]{0,2,1:T(8,128)(2,1)} %copy-done.18) | copy-start | bytes 3932164
  253.7 3.9 %copy-start.3 = (f32[128,3,16,64]{0,3,2,1:T(8,128)S(1)}, f32[128,3,16,64]{0,3,2,1:T(8,128)}, u32[]{:S(2)}) copy-start(f32[128,3,16,64]{0,3,2,1:T(8,128)} %copy-done.1) | copy-start | bytes 4718596
  258.5 12.0 %copy-start.8 = (bf16[128,1024]{1,0:T(8,128)(2,1)S(1)}, bf16[128,1024]{1,0:T(8,128)(2,1)}, u32[]{:S(2)}) copy-start(bf16[128,1024]{1,0:T(8,128)(2,1)} %copy-done.7) | copy-start | bytes 786436
  258.6 12.7 %copy-start.12 = (bf16[640,16,64]{0,2,1:T(8,128)(2,1)S(1)}, bf16[640,16,64]{0,2,1:T(8,128)(2,1)}, u32[]{:S(2)}) copy-start(bf16[640,16,64]{0,2,1:T(8,128)(2,1)} %copy-done.11) | copy-start | bytes 3932164
  259.0 15.5 %collective-permute-start.6 = (bf16[2,128,1024]{1,2,0:T(8,128)(2,1)S(1)}, bf16[2,128,1024]{1,2,0:T(8,128)(2,1)S(1)}, u32[]{:S(2)}, u32[]{:S(2)}) collective-permute-start(bf16[2,128,1024]{1,2,0:T(8,128)(2,1)S(1)} %get-tuple-element.72), channel_id=1, source_target_pairs={{1,0},{2,1},{3,2},{4,3},{5,4},{6,5},{7,6},{8,7},{9,8},{10,9},{11,1... | collective-permute-start | bytes 1572872 | tf_op jit(solution)/shard_map/ppermute | solution.py:19
  263.3 16.7 %collective-permute-start.9 = (bf16[2,128,1024]{1,2,0:T(8,128)(2,1)S(1)}, bf16[2,128,1024]{1,2,0:T(8,128)(2,1)S(1)}, u32[]{:S(2)}, u32[]{:S(2)}) collective-permute-start(bf16[2,128,1024]{1,2,0:T(8,128)(2,1)S(1)} %get-tuple-element.73), channel_id=1, source_target_pairs={{4,0},{5,1},{6,2},{7,3},{8,4},{9,5},{10,6},{11,7},{12,8},{13,9},{1... | collective-permute-start | bytes 1572872 | tf_op jit(solution)/shard_map/ppermute | solution.py:19
  265.2 28.5 %collective-permute-start.8 = (bf16[2,128,1024]{1,2,0:T(8,128)(2,1)S(1)}, bf16[2,128,1024]{1,2,0:T(8,128)(2,1)S(1)}, u32[]{:S(2)}, u32[]{:S(2)}) collective-permute-start(bf16[2,128,1024]{1,2,0:T(8,128)(2,1)S(1)} %get-tuple-element.74), channel_id=1, source_target_pairs={{3,0},{4,1},{5,2},{6,3},{7,4},{8,5},{9,6},{10,7},{11,8},{12,9},{13... | collective-permute-start | bytes 1572872 | tf_op jit(solution)/shard_map/ppermute | solution.py:19
  267.1 34.6 %collective-permute-start.7 = (bf16[2,128,1024]{1,2,0:T(8,128)(2,1)S(1)}, bf16[2,128,1024]{1,2,0:T(8,128)(2,1)S(1)}, u32[]{:S(2)}, u32[]{:S(2)}) collective-permute-start(bf16[2,128,1024]{1,2,0:T(8,128)(2,1)S(1)} %get-tuple-element.75), channel_id=1, source_target_pairs={{2,0},{3,1},{4,2},{5,3},{6,4},{7,5},{8,6},{9,7},{10,8},{11,9},{12,... | collective-permute-start | bytes 1572872 | tf_op jit(solution)/shard_map/ppermute | solution.py:19
  271.3 31.5 %slice-start = ((s8[6291456]{0:T(1024)(128)(4,1)}), s8[2097152]{0:T(1024)(128)(4,1)S(1)}, s32[]{:S(2)}) async-start(s8[6291456]{0:T(1024)(128)(4,1)} %bitcast.178), calls=%async_computation.6 | async-start | bytes 4194304
  272.4 30.4 %slice-start.1 = ((s8[6291456]{0:T(1024)(128)(4,1)}), s8[4194304]{0:T(1024)(128)(4,1)S(1)}, s32[]{:S(2)}) async-start(s8[6291456]{0:T(1024)(128)(4,1)} %bitcast.178), calls=%async_computation.7 | async-start | bytes 8388608
  (9 other events, 9.4 us)
Sparse Core Ops, SparseCore 0:
  159.4 52.2 reduce-scatter.5
  219.2 10.6 reduce-scatter.7
  232.1 9.9 reduce-scatter.3
where the time goes:
time: 313 us; the launch traced here: 312 us
  waiting for transfers between devices  121 us (39%)
  blocking collectives  51.4 us (16%)
  local copies, waits for them, and re-layouts  38.6 us (12%)
  matrix products  37.7 us (12%)
  starting transfers between devices  30.5 us (10%)
  other arithmetic  17.8 us (6%)
  between operations  14.6 us (5%)
    ppermute x10, waiting for transfers between devices, from_behind(): lax.ppermute(value, axis, [(source, source + steps) for source in range(f...  51.4 us
    reduce_scatter x1, waiting for transfers between devices, per_device(): lax.psum_scatter(key_terms.astype(jnp.bfloat16), 'seq', scatter_dimension...  48 us
    ppermute x10, starting transfers between devices, from_behind(): lax.ppermute(value, axis, [(source, source + steps) for source in range(f...  30.2 us
    all_gather x1, blocking collectives, per_device(): lax.all_gather(value_two.reshape(group_size, local_width), 'seq', axis=0,...  23.1 us
    all_gather x1, blocking collectives, per_device(): lax.all_gather(key_two.reshape(group_size, local_width), 'seq', axis=0, t...  21.3 us
    reduce_scatter x2, waiting for transfers between devices, sum_heads(): lax.psum_scatter(rows.astype(jnp.bfloat16), 'sub', scatter_dimension=0, t...  21.3 us
    unnamed x67, local copies, waits for them, and re-layouts  17.6 us
    dot_general x2, matrix products, project_rows(): jnp.dot(normed_b, weight.reshape(weight.shape[0], 3 * local_width), prefe...  7.96 us
  transfers between devices with their start and end apart: 13, of which 10 were waited for; matrix products, arithmetic and copies ran while one was open for 6% of the time, Pallas kernels for 0%

commit v1 on v0

v1 whole, which is shorter than its diff:
```python
import functools

import jax
import jax.numpy as jnp
from jax import lax
from jax.experimental import pallas as pl
from jax.experimental.pallas import tpu as pltpu
from jax.sharding import PartitionSpec as P

D = 1024
HEADS = 16
HEAD_DIM = 64
WINDOW = 512
POOL = 16
EPS = 1e-06
F32 = jnp.float32
BF16 = jnp.bfloat16
MESH = pl.DeviceIdType.MESH
PAIR = 2 * HEAD_DIM
SCALE = HEAD_DIM ** (-0.5)
VMEM = pl.BlockSpec(memory_space=pltpu.VMEM)
ANY = pl.BlockSpec(memory_space=pl.ANY)
SMEM = pl.BlockSpec(memory_space=pltpu.SMEM)


def dot(a, b):
    return jnp.dot(a, b, preferred_element_type=F32)


def dot_nt(a, b):
    return lax.dot_general(a, b, (((1,), (1,)), ((), ())), preferred_element_type=F32)


def dot_tn(a, b):
    return lax.dot_general(a, b, (((0,), (0,)), ((), ())), preferred_element_type=F32)


def split(x):
    hi = x.astype(BF16)
    return hi, (x - hi.astype(F32)).astype(BF16)


def iota(shape, axis):
    return lax.broadcasted_iota(jnp.int32, shape, axis)


def head_sum(x):
    group = (iota((x.shape[1], 128), 0) // HEAD_DIM == iota((x.shape[1], 128), 1)).astype(F32).astype(BF16)
    hi, lo = split(x)
    return dot(hi, group) + dot(lo, group)


def head_spread(f, width):
    group = (iota((128, width), 1) // HEAD_DIM == iota((128, width), 0)).astype(F32).astype(BF16)
    hi, lo = split(f)
    return dot(hi, group) + dot(lo, group)


def head_rms(raw):
    factor = lax.rsqrt(head_sum(raw * raw) / HEAD_DIM + EPS)
    factor = head_spread(factor, raw.shape[1])
    return raw * factor, factor


def head_back(grad, unit, factor):
    return factor * (grad - unit * head_spread(head_sum(unit * grad) / HEAD_DIM, grad.shape[1]))


def rms_rows(x):
    factor = lax.rsqrt(jnp.mean(x * x, axis=-1, keepdims=True) + EPS)
    return x * factor, factor


def row_back(grad, normed, factor):
    return factor * (grad - normed * jnp.mean(normed * grad, axis=-1, keepdims=True))


def both(pair):
    low = iota(pair.shape, 1) < HEAD_DIM
    wide = pair.astype(F32)
    return jnp.concatenate([jnp.where(low, wide, 0.0), jnp.where(low, 0.0, wide)]).astype(BF16)


def pick(stacked):
    half = stacked.shape[0] // 2
    low = iota((half, PAIR), 1) < HEAD_DIM
    return jnp.where(low, stacked[:half], stacked[half:])


def place():
    subs = lax.axis_size("sub")
    count = lax.axis_size("seq") * subs
    me = lax.axis_index("seq") * subs + lax.axis_index("sub")
    return me, count, subs


def coords(index, subs):
    return (index // subs, index % subs)


def greet_all():
    me, count, subs = place()
    barrier = pltpu.get_barrier_semaphore()

    @pl.loop(1, count)
    def _(k):
        pl.semaphore_signal(
            barrier, inc=1, device_id=coords((me + k) % count, subs), device_id_type=MESH
        )

    pl.semaphore_wait(barrier, count - 1)


def remote(src, dst, send, recv, target, subs):
    return pltpu.make_async_remote_copy(
        src_ref=src, dst_ref=dst, send_sem=send, recv_sem=recv,
        device_id=coords(target, subs), device_id_type=MESH,
    )


class Spread:
    def __init__(self, src, dst, sends, recvs, local):
        self.me, self.count, self.subs = place()
        self.args = (src, dst, sends, recvs, local)

    def copy(self, k):
        src, dst, sends, recvs, _ = self.args
        target = (self.me + k) % self.count
        return remote(src, dst.at[self.me], sends.at[k], recvs.at[k], target, self.subs)

    def start(self):
        src, dst, _, _, local = self.args

        @pl.loop(1, self.count)
        def _(k):
            self.copy(k).start()

        pltpu.make_async_copy(src, dst.at[self.me], local).start()

    def wait(self):
        src, dst, sends, recvs, local = self.args

        @pl.loop(1, self.count)
        def _(k):
            self.copy(k).wait_send()
            came = (self.me + self.count - k) % self.count
            remote(src, dst.at[came], sends.at[k], recvs.at[k], came, self.subs).wait_recv()

        pltpu.make_async_copy(src, dst.at[self.me], local).wait()


class Shift:
    def __init__(self, src, dst, send, recv, distance):
        me, count, subs = place()
        self.me, self.subs, self.target = me, subs, me + distance
        self.args = (src, dst, send, recv)
        self.sends = (me + distance >= 0) & (me + distance < count)
        self.gets = (me - distance >= 0) & (me - distance < count)
        self.copy = remote(src, dst, send, recv, jnp.clip(me + distance, 0, count - 1), subs)

    def start(self):
        @pl.when(self.sends)
        def _():
            self.copy.start()

    def wait(self):
        @pl.when(self.sends)
        def _():
            self.copy.wait_send()

        @pl.when(self.gets)
        def _():
            self.copy.wait_recv()


def comm(body, outs, scratch, ident, specs, *args):
    return pl.pallas_call(
        body,
        out_shape=outs,
        in_specs=specs,
        out_specs=jax.tree.map(lambda _: ANY, outs),
        scratch_shapes=scratch,
        compiler_params=pltpu.CompilerParams(collective_id=ident, has_side_effects=True),
    )(*args)


def local_call(body, outs, *args, smem=True):
    return pl.pallas_call(
        body,
        out_shape=outs,
        in_specs=[SMEM] + [VMEM] * (len(args) - 1),
        out_specs=jax.tree.map(lambda _: VMEM, outs),
        compiler_params=pltpu.CompilerParams(vmem_limit_bytes=60 * 1024 * 1024),
    )(*args)


def first_exchange(hops, x_ref, cg_ref, before, after, cg_all, sends, recvs, ag_send, ag_recv, local):
    greet_all()
    spread = Spread(cg_ref, cg_all, ag_send, ag_recv, local)
    moves = []
    for d in range(1, hops + 1):
        moves.append(Shift(x_ref, before.at[hops - d], sends.at[d - 1], recvs.at[d - 1], d))
        moves.append(
            Shift(x_ref, after.at[d - 1], sends.at[hops + d - 1], recvs.at[hops + d - 1], -d)
        )
    for move in moves:
        move.start()
    spread.start()
    for move in moves:
        move.wait()
    spread.wait()


def second_exchange(
    hops, hidden_ref, cot_ref, pooled_all, cot_after, tail, pooled, sends, recvs, ag_send, ag_recv, local
):
    me, count, subs = place()
    rows = hidden_ref.shape[0]
    outs = rows // POOL
    greet_all()
    carry = Shift(hidden_ref.at[pl.ds(rows - POOL, POOL)], tail, sends.at[hops], recvs.at[hops], 1)
    carry.start()
    back = iota((outs, rows), 0) * POOL - iota((outs, rows), 1)
    part = dot(((back >= 0) & (back < POOL)).astype(F32).astype(BF16), hidden_ref[...])
    carry.wait()
    lead = (iota((outs, POOL), 0) == 0) & (iota((outs, POOL), 1) > 0)
    tail_rows = jnp.where(me > 0, tail[...].astype(F32), 0.0).astype(BF16)
    part = part + dot(lead.astype(F32).astype(BF16), tail_rows)
    pooled[...] = (part / POOL).astype(BF16)
    spread = Spread(pooled, pooled_all, ag_send, ag_recv, local)
    spread.start()
    moves = [
        Shift(cot_ref, cot_after.at[d - 1], sends.at[d - 1], recvs.at[d - 1], -d)
        for d in range(1, hops + 1)
    ]
    for move in moves:
        move.start()
    spread.wait()
    for move in moves:
        move.wait()


def third_exchange(far, mixed_all, grad_all, mixed_in, grad_in, sends, recvs, local):
    me, count, subs = place()
    mine = lax.axis_index("sub")
    seq = lax.axis_index("seq")
    outs = mixed_in.shape[1]
    barrier = pltpu.get_barrier_semaphore()
    for k in range(1, subs):
        pl.semaphore_signal(
            barrier, inc=1, device_id=(seq, (mine + k) % subs), device_id_type=MESH
        )
    pl.semaphore_wait(barrier, subs - 1)
    copies = []
    for k in range(1, subs):
        target = seq * subs + (mine + k) % subs
        start = pl.multiple_of(target * outs, outs)
        pieces = (
            (mixed_all.at[pl.ds(start, outs)], mixed_in.at[k]),
            (grad_all.at[pl.ds(start, far)], grad_in.at[k]),
        )
        for which, (src, dst) in enumerate(pieces):
            copies.append(remote(src, dst, sends.at[2 * k + which], recvs.at[2 * k + which], target, subs))
    for copy in copies:
        copy.start()
    start = pl.multiple_of(me * outs, outs)
    own = [
        pltpu.make_async_copy(mixed_all.at[pl.ds(start, outs)], mixed_in.at[0], local.at[0]),
        pltpu.make_async_copy(grad_all.at[pl.ds(start, far)], grad_in.at[0], local.at[1]),
    ]
    for copy in own:
        copy.start()
    for copy in copies + own:
        copy.wait()


def fourth_exchange(hops, stats_ref, after, sends, recvs):
    me, count, subs = place()
    barrier = pltpu.get_barrier_semaphore()
    for d in range(1, hops + 1):
        for other in (me - d, me + d):

            @pl.when((other >= 0) & (other < count))
            def _():
                pl.semaphore_signal(
                    barrier, inc=1, device_id=coords(jnp.clip(other, 0, count - 1), subs),
                    device_id_type=MESH,
                )

    pl.semaphore_wait(barrier, jnp.minimum(me, hops) + jnp.minimum(count - 1 - me, hops))

    moves = [
        Shift(stats_ref, after.at[d - 1], sends.at[d - 1], recvs.at[d - 1], -d)
        for d in range(1, hops + 1)
    ]
    for move in moves:
        move.start()
    for move in moves:
        move.wait()


def window_mask(rows, keys, anchor):
    gap = keys - rows + iota((rows, keys), 0) - iota((rows, keys), 1)
    return (gap >= 0) & (gap < WINDOW) & (anchor - (keys - rows) + iota((rows, keys), 1) >= 0)


def fine_forward(
    pos, before, x_ref, after, w_ref, out_w,
    q_all, k_all, v_all, unit_q, unit_k, scale_q, scale_k, tot_ref, att_ref, hidden_ref,
):
    rows = x_ref.shape[0]
    margin = before.shape[0]
    anchor = pos[0] * rows
    own = x_ref[...].astype(F32)
    prev = before[...].astype(F32)
    prev = jnp.where(anchor - margin + iota(prev.shape, 0) >= 0, prev, 0.0)
    nxt = after[...].astype(F32)
    nxt = jnp.where(anchor + rows + iota(nxt.shape, 0) < pos[1] * rows, nxt, 0.0)
    own_b = rms_rows(own)[0].astype(BF16)
    past_b = jnp.concatenate([rms_rows(prev)[0].astype(BF16), own_b])
    next_b = jnp.concatenate([own_b, rms_rows(nxt)[0].astype(BF16)])
    unit, factor = head_rms(dot(next_b, w_ref[0]))
    q_all[...] = unit.astype(BF16)
    unit_q[...] = unit[:rows]
    scale_q[...] = factor[:rows]
    unit, factor = head_rms(dot(past_b, w_ref[1]))
    k_all[...] = unit.astype(BF16)
    unit_k[...] = unit[margin:]
    scale_k[...] = factor[margin:]
    v_all[...] = dot(past_b, w_ref[2]).astype(BF16)
    mask = window_mask(rows, margin + rows, anchor)
    mask = jnp.concatenate([mask.astype(F32)] * 2) > 0
    lane = iota((rows, 128), 1)
    totals = jnp.ones((rows, 128), F32)
    for p in range(HEADS // 2):
        cols = pl.ds(p * PAIR, PAIR)
        s = dot_nt(both(q_all[pl.ds(0, rows), cols]), k_all[:, cols]) * SCALE
        e = jnp.where(mask, jnp.exp(s), 0.0)
        t = jnp.sum(e, axis=-1, keepdims=True)
        prob = (e * (1.0 / t)).astype(BF16)
        att_ref[:, cols] = pick(dot(prob, v_all[:, cols])).astype(BF16)
        totals = jnp.where(lane == 2 * p, t[:rows], totals)
        totals = jnp.where(lane == 2 * p + 1, t[rows:], totals)
    tot_ref[...] = totals
    hidden_ref[...] = (own + dot(att_ref[...], out_w[...])).astype(BF16)


def coarse_level(pos, pooled_ref, cg_ref, w_ref, out_w, mixed_ref, grad_ref):
    count, width = pooled_ref.shape[0], w_ref.shape[2]
    normed_b = rms_rows(pooled_ref[...].astype(F32))[0].astype(BF16)
    uq, fq = head_rms(dot(normed_b, w_ref[0]))
    uk, fk = head_rms(dot(normed_b, w_ref[1]))
    qb, kb = uq.astype(BF16), uk.astype(BF16)
    vb = dot(normed_b, w_ref[2]).astype(BF16)
    gb = dot_nt(cg_ref[...], out_w[...]).astype(BF16)
    block = min(count, 256)
    att_p, dq_p, dk_p, dv_p = [], [], [], []
    for p in range(width // PAIR):
        cols = slice(p * PAIR, (p + 1) * PAIR)
        att_b, dq_b, dk, dv = [], [], None, None
        kp, vp = kb[:, cols], vb[:, cols]
        for b in range(count // block):
            rows = slice(b * block, (b + 1) * block)
            qs, gs = both(qb[rows, cols]), both(gb[rows, cols])
            s = dot_nt(qs, kp) * SCALE
            where = iota((2 * block, count), 0) % block + b * block >= iota((2 * block, count), 1)
            e = jnp.where(where, jnp.exp(s), 0.0)
            full = e * (1.0 / jnp.sum(e, axis=-1, keepdims=True))
            prob = full.astype(BF16)
            att = pick(dot(prob, vp)).astype(BF16)
            att_b.append(att)
            att2 = jnp.concatenate([att.astype(F32)] * 2)
            delta = jnp.sum(gs.astype(F32) * att2, axis=-1, keepdims=True)
            ds = (full * (dot_nt(gs, vp) - delta)).astype(BF16)
            dq_b.append(pick(dot(ds, kp)) * SCALE)
            dk_t, dv_t = dot_tn(ds, qs) * SCALE, dot_tn(prob, gs)
            dk = dk_t if dk is None else dk + dk_t
            dv = dv_t if dv is None else dv + dv_t
        att_p.append(jnp.concatenate(att_b))
        dq_p.append(jnp.concatenate(dq_b))
        dk_p.append(dk)
        dv_p.append(dv)
    join = lambda parts: jnp.concatenate(parts, axis=1)
    mixed_ref[...] = dot(join(att_p), out_w[...]).astype(BF16)
    dq = head_back(join(dq_p), uq, fq).astype(BF16)
    dk = head_back(join(dk_p), uk, fk).astype(BF16)
    dv = join(dv_p).astype(BF16)
    total = dot_nt(dq, w_ref[0]) + dot_nt(dk, w_ref[1]) + dot_nt(dv, w_ref[2])
    grad_ref[pl.ds(0, count), :] = total.astype(BF16)
    extra = grad_ref.shape[0] - count
    grad_ref[pl.ds(count, extra), :] = jnp.zeros((extra, D), BF16)


def middle(
    pos, hidden_ref, mixed_in, grad_in, pooled_ref, cg_ref, cot_ref, cot_after, att_ref, tot_ref, out_w,
    output_ref, hg_ref, g_all, delta_ref, stats_ref,
):
    rows = hidden_ref.shape[0]
    outs = rows // POOL
    ahead = cot_after.shape[0]
    far = grad_in.shape[1]
    start = pos[0] * rows
    pooled = pooled_ref[...].astype(F32)
    mixed = jnp.sum(mixed_in[...].astype(F32), axis=0)
    state = (pooled[:outs] + mixed).astype(BF16)
    onto = (iota((rows, outs), 0) // POOL == iota((rows, outs), 1)).astype(F32).astype(BF16)
    output_ref[...] = (hidden_ref[...].astype(F32) + dot(onto, state)).astype(BF16)
    nxt = cot_after[...].astype(F32)
    nxt = jnp.where(start + rows + iota(nxt.shape, 0) < pos[1] * rows, nxt, 0.0)
    cot = jnp.concatenate([cot_ref[...].astype(F32), nxt])
    length = rows + ahead
    near = length // POOL
    groups = (iota((near, length), 1) // POOL == iota((near, length), 0)).astype(F32).astype(BF16)
    cg = jnp.concatenate([dot(groups, cot.astype(BF16)), cg_ref[...].astype(F32)[near:]])
    ng = jnp.sum(grad_in[...].astype(F32), axis=0)
    normed, factor = rms_rows(pooled)
    pg = (cg + row_back(ng, normed, factor)) / POOL
    pg = jnp.where(pos[0] * outs + iota(pg.shape, 0) < pos[1] * outs, pg, 0.0)
    lift = ((iota((length, far), 0) + POOL - 1) // POOL == iota((length, far), 1)).astype(F32).astype(BF16)
    hi, lo = split(pg)
    hidden_grad = cot + dot(lift, hi) + dot(lift, lo)
    hg_ref[...] = hidden_grad[:rows]
    g_all[...] = dot_nt(hidden_grad.astype(BF16), out_w[...]).astype(BF16)
    delta = head_sum(g_all[pl.ds(0, rows), :].astype(F32) * att_ref[...].astype(F32))
    delta_ref[...] = delta
    stats_ref[pl.ds(0, HEADS), :] = tot_ref[...].T[:HEADS]
    stats_ref[pl.ds(HEADS, HEADS), :] = delta.T[:HEADS]


def fine_backward(
    pos, x_ref, w_ref, q_all, k_all, v_all, g_all, own_stats, after, tot_ref, delta_ref,
    unit_q, unit_k, scale_q, scale_k, hg_ref, grad_ref,
):
    rows = x_ref.shape[0]
    hops = after.shape[0]
    margin = k_all.shape[0] - rows
    length = q_all.shape[0]
    anchor = pos[0] * rows
    mask = window_mask(rows, margin + rows, anchor)
    mask = jnp.concatenate([mask.astype(F32)] * 2) > 0
    gap = iota((rows, length), 1) - iota((rows, length), 0)
    mask_t = (gap >= 0) & (gap < WINDOW) & (anchor + iota((rows, length), 1) < pos[1] * rows)
    stats = jnp.concatenate([own_stats[...]] + [after[d] for d in range(hops)], axis=1)
    stats = jnp.where(anchor + iota(stats.shape, 1) < pos[1] * rows, stats, 1.0)
    totals, deltas = tot_ref[...], delta_ref[...]
    dq_p, dk_p, dv_p = [], [], []
    for p in range(HEADS // 2):
        cols = pl.ds(p * PAIR, PAIR)
        kp, vp, qp, gp = k_all[:, cols], v_all[:, cols], q_all[:, cols], g_all[:, cols]
        s = dot_nt(both(qp[:rows]), kp) * SCALE
        e = jnp.where(mask, jnp.exp(s), 0.0)
        column = lambda m: jnp.concatenate([m[:, 2 * p : 2 * p + 1], m[:, 2 * p + 1 : 2 * p + 2]])
        ds = e * (1.0 / column(totals)) * (dot_nt(both(gp[:rows]), vp) - column(deltas))
        dq_p.append(pick(dot(ds.astype(BF16), kp)) * SCALE)
        k_own, v_own = kp[margin:], vp[margin:]
        qs, gs = both(qp), both(gp)
        dk = dv = jnp.zeros((rows, PAIR), F32)
        for h in range(2):
            part = slice(h * length, (h + 1) * length)
            st = dot_nt(k_own, qs[part]) * SCALE
            head = 2 * p + h
            pt = jnp.where(mask_t, jnp.exp(st), 0.0) * (1.0 / stats[head : head + 1])
            dst = pt * (dot_nt(v_own, gs[part]) - stats[HEADS + head : HEADS + head + 1])
            dk = dk + dot(dst.astype(BF16), qs[part])
            dv = dv + dot(pt.astype(BF16), gs[part])
        dk_p.append(dk * SCALE)
        dv_p.append(dv)
    join = lambda parts: jnp.concatenate(parts, axis=1)
    dq = head_back(join(dq_p), unit_q[...], scale_q[...]).astype(BF16)
    dk = head_back(join(dk_p), unit_k[...], scale_k[...]).astype(BF16)
    dv = join(dv_p).astype(BF16)
    total = dot_nt(dq, w_ref[0]) + dot_nt(dk, w_ref[1]) + dot_nt(dv, w_ref[2])
    normed, factor = rms_rows(x_ref[...].astype(F32))
    grad_ref[...] = (hg_ref[...] + row_back(total, normed, factor)).astype(BF16)


def per_device(tokens, cotangent, fine_qkv, fine_out, coarse_qkv, coarse_out):
    rows = tokens.shape[0]
    hops = -(-WINDOW // rows)
    outs = rows // POOL
    me, count, subs = place()
    pos = jnp.stack([me, jnp.int32(count)]).astype(jnp.int32)
    far = (hops + 2) * outs
    shape = jax.ShapeDtypeStruct
    dma = pltpu.SemaphoreType.DMA
    fine_w = jnp.transpose(fine_qkv, (1, 0, 2))
    coarse_w = jnp.transpose(coarse_qkv, (1, 0, 2))
    coarse_grad = cotangent.astype(F32).reshape(outs, POOL, D).sum(axis=1).astype(BF16)
    before, after, cg_all = comm(
        functools.partial(first_exchange, hops),
        (shape((hops, rows, D), BF16), shape((hops, rows, D), BF16), shape((count, outs, D), BF16)),
        [dma((2 * hops,)), dma((2 * hops,)), dma((count,)), dma((count,)), dma],
        0, [VMEM, VMEM], tokens, coarse_grad,
    )
    length = (hops + 1) * rows
    flat = lambda a: a.reshape(-1, D)
    q_all, k_all, v_all, unit_q, unit_k, scale_q, scale_k, totals, attended, hidden = local_call(
        fine_forward,
        [shape((length, D), BF16)] * 3 + [shape((rows, D), F32)] * 4
        + [shape((rows, 128), F32)] + [shape((rows, D), BF16)] * 2,
        pos, flat(before), tokens, flat(after), fine_w, fine_out,
    )
    pooled_all, cot_after = comm(
        functools.partial(second_exchange, hops),
        (shape((count, outs, D), BF16), shape((hops, rows, D), BF16)),
        [pltpu.VMEM((POOL, D), BF16), pltpu.VMEM((outs, D), BF16), dma((hops + 1,)), dma((hops + 1,)),
         dma((count,)), dma((count,)), dma],
        1, [VMEM, VMEM], hidden, cotangent,
    )
    pooled_all, cg_all = flat(pooled_all), flat(cg_all)
    mixed_all, grad_all = local_call(
        coarse_level,
        [shape((count * outs, D), BF16), shape((count * outs + far, D), BF16)],
        pos, pooled_all, cg_all, coarse_w, coarse_out,
    )
    mixed_in, grad_in = comm(
        functools.partial(third_exchange, far),
        (shape((subs, outs, D), BF16), shape((subs, far, D), BF16)),
        [dma((2 * subs,)), dma((2 * subs,)), dma((2,))],
        2, [VMEM, VMEM], mixed_all, grad_all,
    )
    tail = lambda a: lax.dynamic_slice_in_dim(jnp.pad(a, ((0, far), (0, 0))), me * outs, far)
    output, hidden_grad, g_all, delta, stats = local_call(
        middle,
        [shape((rows, D), BF16), shape((rows, D), F32), shape((length, D), BF16),
         shape((rows, 128), F32), shape((2 * HEADS, rows), F32)],
        pos, hidden, mixed_in, grad_in, tail(pooled_all), tail(cg_all), cotangent, flat(cot_after),
        attended, totals, fine_out,
    )
    stats_after = comm(
        functools.partial(fourth_exchange, hops),
        shape((hops, 2 * HEADS, rows), F32),
        [dma((hops,)), dma((hops,))],
        3, [VMEM], stats,
    )
    grad_tokens = local_call(
        fine_backward, shape((rows, D), BF16),
        pos, tokens, fine_w, q_all, k_all, v_all, g_all, stats, stats_after, totals, delta,
        unit_q, unit_k, scale_q, scale_k, hidden_grad,
    )
    return (output, grad_tokens)


def solution(mesh):
    placed = (
        P(("seq", "sub"), None),
        P(("seq", "sub"), None),
        P(),
        P(),
        P(None, None, "sub"),
        P("sub", None),
    )
    return jax.shard_map(
        per_device,
        mesh=mesh,
        in_specs=placed,
        out_specs=(P(("seq", "sub"), None), P(("seq", "sub"), None)),
        check_vma=False,
    )
```

time: 313 us -> 155 us (0.50)
  Pallas kernels: 0 us -> 150 us
  waiting for transfers between devices: 121 us -> 0 us
  blocking collectives: 51.4 us -> 0 us
  matrix products: 37.7 us -> 0 us
  local copies, waits for them, and re-layouts: 38.6 us -> 1.63 us
  starting transfers between devices: 30.5 us -> 0 us
  other arithmetic: 17.8 us -> 2.23 us
  between operations: 14.6 us -> 0.69 us
    pallas_call x0 -> x8, Pallas kernels: none -> 150 us  [the longest x4 100 us: comm(): pl.pallas_call(body, out_shape=outs, in_specs=specs, out_specs=jax.tree.m...]
    reduce_scatter x3 -> x0, waiting for transfers between devices: 69.3 us -> none  [the longest x1 48 us: per_device(): lax.psum_scatter(key_terms.astype(jnp.bfloat16), 'seq', scatter_dimension...]
    all_gather x4 -> x0, blocking collectives: 51.4 us -> none  [the longest x1 23.1 us: per_device(): lax.all_gather(value_two.reshape(group_size, local_width), 'seq', axis=0,...]
    ppermute x10 -> x0, waiting for transfers between devices: 51.4 us -> none  [from_behind(): lax.ppermute(value, axis, [(source, source + steps) for source in range(f...]
    dot_general x20 -> x0, matrix products: 37.7 us -> none  [the longest x2 7.96 us: project_rows(): jnp.dot(normed_b, weight.reshape(weight.shape[0], 3 * local_width), prefe...]
    ppermute x10 -> x0, starting transfers between devices: 30.2 us -> none  [from_behind(): lax.ppermute(value, axis, [(source, source + steps) for source in range(f...]
    unnamed x67 -> x2, local copies, waits for them, and re-layouts: 17.6 us -> 0.01 us
    slice x17 -> x0, local copies, waits for them, and re-layouts: 7.34 us -> none  [the longest x4 4.29 us: per_device(): pieces[0]]
  transfers between devices with their start and end apart: 13 -> 0, of which waited for: 10 -> 0; matrix products, arithmetic and copies ran while one was open for 6% -> 0% of each run, Pallas kernels for 0% -> 0%
where the time goes in v1:
time: 155 us; the launch traced here: 154 us
  Pallas kernels  150 us (97%)
  other arithmetic  2.23 us (1%)
  local copies, waits for them, and re-layouts  1.63 us (1%)
    pallas_call x4, Pallas kernels, comm(): pl.pallas_call(body, out_shape=outs, in_specs=specs, out_specs=jax.tree.m...  100 us
    pallas_call x4, Pallas kernels, local_call(): pl.pallas_call(body, out_shape=outs, in_specs=[SMEM] + [VMEM] * (len(args...  49.7 us

profile of v1, /device:TPU:5, one launch (start us, length us, event | category | flops | bytes accessed | tf_op | source)
XLA Modules:
  0.0 154.2 jit_solution(14439326791435881134)
XLA Ops:
  0.6 0.6 pad_add_fusion.pos
  1.2 1.7 %bitcast_reduce_fusion.cg_ref = bf16[8,1024]{1,0:T(8,128)(2,1)} fusion(bf16[128,1024]{1,0:T(8,128)(2,1)} %cot_ref.3), kind=kLoop, calls=%fused_computation.2 | loop fusion | flops 122880 | bytes 278528 | tf_op jit(solution)/shard_map/reduce_sum | solution.py:488
  2.9 42.7 %shard_map.77 = (bf16[4,128,1024]{2,1,0:T(8,128)(2,1)}, bf16[4,128,1024]{2,1,0:T(8,128)(2,1)}, bf16[32,8,1024]{2,1,0:T(8,128)(2,1)}) custom-call(bf16[128,1024]{1,0:T(8,128)(2,1)} %x_ref.5, bf16[8,1024]{1,0:T(8,128)(2,1)} %bitcast_reduce_fusion.cg_ref), custom_call_target="tpu_custom_call" | custom-call | tf_op jit(solution)/shard_map/pallas_call | solution.py:177
  45.6 0.0 copy-start
  45.6 17.8 %shard_map.78 = (bf16[640,1024]{1,0:T(8,128)(2,1)}, bf16[640,1024]{1,0:T(8,128)(2,1)}, bf16[640,1024]{1,0:T(8,128)(2,1)}, f32[128,1024]{1,0:T(8,128)}, f32[128,1...) custom-call(s32[2]{0:T(128)} %pad_add_fusion.pos, ...), custom_call_target="tpu_custom_call" | custom-call | tf_op jit(solution)/shard_map/pallas_call | solution.py:188
  63.4 36.9 %shard_map.79 = (bf16[32,8,1024]{2,1,0:T(8,128)(2,1)}, bf16[4,128,1024]{2,1,0:T(8,128)(2,1)}) custom-call(bf16[128,1024]{1,0:T(8,128)(2,1)} %get-tuple-element.28.hidden_ref, bf16[128,1024]{1,0:T(8,128)(2,1)} %cot_ref.3), custom_call_target="tpu_custom_call" | custom-call | tf_op jit(solution)/shard_map/pallas_call | solution.py:177
  100.3 0.0 copy-done
  100.3 1.6 %pad_dynamic-slice_fusion = (bf16[48,1024]{1,0:T(8,128)(2,1)}, bf16[48,1024]{1,0:T(8,128)(2,1)}) fusion(s32[]{:T(128)S(6)} %select_n.4, bf16[256,1024]{1,0:T(8,128)(2,1)S(1)} %bitcast.14, bf16[256,1024]{1,0:T(8,128)(2,1)} %bitcast.15), kind=kLoop, calls=%fused_computation | loop fusion | bytes 1245188 | tf_op jit(solution)/shard_map/dynamic_slice | solution.py:522
  101.9 10.5 %shard_map.80 = (bf16[256,1024]{1,0:T(8,128)(2,1)}, bf16[304,1024]{1,0:T(8,128)(2,1)}) custom-call(s32[2]{0:T(128)} %pad_add_fusion.pos, bf16[256,1024]{1,0:T(8,128)(2,1)} %bitcast.16, bf16[256,1024]{1,0:T(8,128)(2,1)} %bitcast.13, bf16[3,1024,512]{2,1,0:T(8,128)(2,1)} %bitcast.12, bf16[512,1024]{1,0:T(8,128)(2,1)} %out_w.4), custom_call_target="tpu_custom_call" | custom-call | tf_op jit(solution)/shard_map/pallas_call | solution.py:188
  112.4 5.1 %shard_map.81 = (bf16[2,8,1024]{2,1,0:T(8,128)(2,1)}, bf16[2,48,1024]{2,1,0:T(8,128)(2,1)}) custom-call(bf16[256,1024]{1,0:T(8,128)(2,1)} %get-tuple-element.31.mixed_all, bf16[304,1024]{1,0:T(8,128)(2,1)} %get-tuple-element.32.grad_all), custom_call_target="tpu_custom_call" | custom-call | tf_op jit(solution)/shard_map/pallas_call | solution.py:177
  117.4 6.0 %shard_map.82 = (bf16[128,1024]{1,0:T(8,128)(2,1)}, f32[128,1024]{1,0:T(8,128)}, bf16[640,1024]{1,0:T(8,128)(2,1)}, f32[128,128]{1,0:T(8,128)}, f32[32,128]{1,0:T(8,128)}) custom-call(s32[2]{0:T(128)} %pad_add_fusion.pos, bf16[128,1024]{1,0:T(8,128)(2,1)} %get-tuple-element.28.hidden_ref, bf16[2,8,1024]{2,1,0:T(8,128)(2,1)} %get-tuple-element.33.mixed_in, ...), custom_call_target="tpu_custom_call" | custom-call | tf_op jit(solution)/shard_map/pallas_call | solution.py:188
  123.5 15.3 %shard_map.83.after = f32[4,32,128]{2,1,0:T(8,128)} custom-call(f32[32,128]{1,0:T(8,128)} %get-tuple-element.43.stats_ref.own_stats), custom_call_target="tpu_custom_call" | custom-call | tf_op jit(solution)/shard_map/pallas_call | solution.py:177
  138.8 15.5 %shard_map.84 = bf16[128,1024]{1,0:T(8,128)(2,1)} custom-call(s32[2]{0:T(128)} %pad_add_fusion.pos, bf16[128,1024]{1,0:T(8,128)(2,1)} %x_ref.5, bf16[3,1024,1024]{2,1,0:T(8,128)(2,1)} %bitcast.11, bf16[640,1024]{1,0:T(8,128)(2,1)} %get-tuple-element.39.q_all, bf16[640,1024]{1,0:T(8,128)(2,1)} %get-tuple-element.40.k_all, ...), custom_call_target="tpu_custom_call" | custom-call | tf_op jit(solution)/shard_map/pallas_call | solution.py:188
Async XLA Ops:
  45.6 54.6 %copy-start = (bf16[32,8,1024]{2,1,0:T(8,128)(2,1)S(1)}, bf16[32,8,1024]{2,1,0:T(8,128)(2,1)}, u32[]{:S(2)}) copy-start(bf16[32,8,1024]{2,1,0:T(8,128)(2,1)} %get-tuple-element.30) | copy-start | bytes 1572868

commit v2 on v1

--- a/solution.py
+++ b/solution.py
@@ -119,34 +119,156 @@
 
 
 class Spread:
-    def __init__(self, src, dst, sends, recvs, local):
+    def __init__(self, src, dst, out_sem, mid_sem, last_sem, sent):
         self.me, self.count, self.subs = place()
-        self.args = (src, dst, sends, recvs, local)
-
-    def copy(self, k):
-        src, dst, sends, recvs, _ = self.args
-        target = (self.me + k) % self.count
-        return remote(src, dst.at[self.me], sends.at[k], recvs.at[k], target, self.subs)
+        self.cores = 2 if lax.axis_size("seq") % 2 == 0 else 1
+        self.groups = self.count // self.subs // self.cores
+        self.sub = self.me % self.subs
+        self.core = self.me // self.subs % self.cores
+        self.group = self.me // self.subs // self.cores
+        self.src, self.dst, self.sems, self.sent = src, dst, (out_sem, mid_sem, last_sem), sent
+
+    def index(self, k, core, j):
+        group = (self.group + self.groups - k) % self.groups
+        sub = (self.sub + self.subs - j) % self.subs
+        return (group * self.cores + (self.core + core) % self.cores) * self.subs + sub
+
+    def copy(self, phase, j, k):
+        if phase == 0:
+            spot, source = self.me, self.src
+            target, sem = self.index(self.groups - k, 0, 0), self.sems[0].at[k]
+        elif phase == 1:
+            spot = self.index(k, 0, 0)
+            target, sem = self.index(0, 0, self.subs - j), self.sems[1].at[j, k]
+        else:
+            spot = self.index(k, 0, j)
+            target, sem = self.index(0, 1, 0), self.sems[2].at[j, k]
+        source = self.src if phase == 0 else self.dst.at[spot]
+        return remote(source, self.dst.at[spot], self.sent.at[phase, j, k], sem, target, self.subs)
+
+    def arrive(self, phase, j, k):
+        if phase == 0:
+            spot, sem = self.index(k, 0, 0), self.sems[0].at[k]
+        elif phase == 1:
+            spot, sem = self.index(k, 0, j), self.sems[1].at[j, k]
+        else:
+            spot, sem = self.index(k, 1, j), self.sems[2].at[j, k]
+        other = (self.me + 1) % self.count
+        return remote(self.dst.at[spot], self.dst.at[spot], self.sent.at[phase, j, k], sem, other, self.subs)
+
+    def relay(self, k):
+        for j in range(1, self.subs):
+            self.copy(1, j, k).start()
+        if self.cores > 1:
+            self.copy(2, 0, k).start()
 
     def start(self):
-        src, dst, _, _, local = self.args
-
-        @pl.loop(1, self.count)
+        self.dst[self.me] = self.src[...]
+
+        @pl.loop(1, self.groups)
         def _(k):
-            self.copy(k).start()
-
-        pltpu.make_async_copy(src, dst.at[self.me], local).start()
-
-    def wait(self):
-        src, dst, sends, recvs, local = self.args
-
-        @pl.loop(1, self.count)
+            self.copy(0, 0, k).start()
+
+        self.relay(0)
+
+    def finish(self):
+        @pl.loop(1, self.groups)
         def _(k):
-            self.copy(k).wait_send()
-            came = (self.me + self.count - k) % self.count
-            remote(src, dst.at[came], sends.at[k], recvs.at[k], came, self.subs).wait_recv()
-
-        pltpu.make_async_copy(src, dst.at[self.me], local).wait()
+            self.arrive(0, 0, k).wait_recv()
+            self.relay(k)
+
+        @pl.loop(0, self.groups)
+        def _(k):
+            for j in range(1, self.subs):
+                self.arrive(1, j, k).wait_recv()
+                if self.cores > 1:
+                    self.copy(2, j, k).start()
+
+        @pl.loop(0, self.groups)
+        def _(k):
+            for j in range(self.subs):
+                if self.cores > 1:
+                    self.arrive(2, j, k).wait_recv()
+                    self.copy(2, j, k).wait_send()
+                if j > 0:
+                    self.copy(1, j, k).wait_send()
+
+        @pl.loop(1, self.groups)
+        def _(k):
+            self.copy(0, 0, k).wait_send()
+
+
+def spread_sems(count, subs):
+    cores = 2 if count // subs % 2 == 0 else 1
+    groups = count // subs // cores
+    dma = pltpu.SemaphoreType.DMA
+    return [dma((groups,)), dma((subs, groups)), dma((subs, groups)), dma((3, subs, groups))]
+
+
+class Halo:
+    def __init__(self, src, dst, sends, recvs, hops, sign):
+        self.me, self.count, self.subs = place()
+        self.src, self.dst, self.sends, self.recvs = src, dst, sends, recvs
+        self.hops, self.sign = hops, sign
+        self.paired = lax.axis_size("seq") % 2 == 0
+        far_core = self.me // self.subs % 2
+        self.first = far_core == (0 if sign > 0 else 1)
+
+    def slot(self, d):
+        return self.dst.at[self.hops - d if self.sign > 0 else d - 1]
+
+    def inside(self, index):
+        return (index >= 0) & (index < self.count)
+
+    def cuts(self, d):
+        if not self.paired or d <= self.subs:
+            return self.inside(self.me + self.sign * d)
+        target = self.me + self.sign * d + 2 * self.count * self.subs
+        core = target // self.subs % 2
+        return self.inside(self.me + self.sign * d) & (core == (0 if self.sign > 0 else 1))
+
+    def direct(self, d):
+        target = jnp.clip(self.me + self.sign * d, 0, self.count - 1)
+        return remote(self.src, self.slot(d), self.sends.at[d - 1], self.recvs.at[d - 1], target, self.subs)
+
+    def passed(self, d):
+        target = jnp.clip(self.me + self.sign * self.subs, 0, self.count - 1)
+        to = d + self.subs
+        return remote(
+            self.slot(d), self.slot(to), self.sends.at[self.hops + to - 1], self.recvs.at[to - 1],
+            target, self.subs,
+        )
+
+    def relays(self, d):
+        return self.first & self.inside(self.me - self.sign * d)
+
+    def start(self):
+        for d in range(1, self.hops + 1):
+            @pl.when(self.cuts(d))
+            def _():
+                self.direct(d).start()
+
+    def finish(self):
+        for d in range(1, self.hops + 1):
+            @pl.when(self.inside(self.me - self.sign * d))
+            def _():
+                self.direct(d).wait_recv()
+
+            if self.paired and d + self.subs <= self.hops:
+                @pl.when(self.relays(d))
+                def _():
+                    self.passed(d).start()
+
+    def drain(self):
+        for d in range(1, self.hops + 1):
+            @pl.when(self.cuts(d))
+            def _():
+                self.direct(d).wait_send()
+
+            if self.paired and d + self.subs <= self.hops:
+                @pl.when(self.relays(d))
+                def _():
+                    self.passed(d).wait_send()
 
 
 class Shift:
@@ -173,14 +295,16 @@
             self.copy.wait_recv()
 
 
-def comm(body, outs, scratch, ident, specs, *args):
+def comm(body, outs, scratch, ident, specs, *args, out_specs=None):
     return pl.pallas_call(
         body,
         out_shape=outs,
         in_specs=specs,
-        out_specs=jax.tree.map(lambda _: ANY, outs),
+        out_specs=jax.tree.map(lambda _: ANY, outs) if out_specs is None else out_specs,
         scratch_shapes=scratch,
-        compiler_params=pltpu.CompilerParams(collective_id=ident, has_side_effects=True),
+        compiler_params=pltpu.CompilerParams(
+            collective_id=ident, has_side_effects=True, vmem_limit_bytes=60 * 1024 * 1024
+        ),
     )(*args)
 
 
@@ -194,31 +318,12 @@
     )(*args)
 
 
-def first_exchange(hops, x_ref, cg_ref, before, after, cg_all, sends, recvs, ag_send, ag_recv, local):
-    greet_all()
-    spread = Spread(cg_ref, cg_all, ag_send, ag_recv, local)
-    moves = []
-    for d in range(1, hops + 1):
-        moves.append(Shift(x_ref, before.at[hops - d], sends.at[d - 1], recvs.at[d - 1], d))
-        moves.append(
-            Shift(x_ref, after.at[d - 1], sends.at[hops + d - 1], recvs.at[hops + d - 1], -d)
-        )
-    for move in moves:
-        move.start()
-    spread.start()
-    for move in moves:
-        move.wait()
-    spread.wait()
-
-
-def second_exchange(
-    hops, hidden_ref, cot_ref, pooled_all, cot_after, tail, pooled, sends, recvs, ag_send, ag_recv, local
-):
+def second_exchange(hidden_ref, pooled_all, tail, pooled, send, recv, *sems):
     me, count, subs = place()
     rows = hidden_ref.shape[0]
     outs = rows // POOL
     greet_all()
-    carry = Shift(hidden_ref.at[pl.ds(rows - POOL, POOL)], tail, sends.at[hops], recvs.at[hops], 1)
+    carry = Shift(hidden_ref.at[pl.ds(rows - POOL, POOL)], tail, send, recv, 1)
     carry.start()
     back = iota((outs, rows), 0) * POOL - iota((outs, rows), 1)
     part = dot(((back >= 0) & (back < POOL)).astype(F32).astype(BF16), hidden_ref[...])
@@ -227,17 +332,9 @@
     tail_rows = jnp.where(me > 0, tail[...].astype(F32), 0.0).astype(BF16)
     part = part + dot(lead.astype(F32).astype(BF16), tail_rows)
     pooled[...] = (part / POOL).astype(BF16)
-    spread = Spread(pooled, pooled_all, ag_send, ag_recv, local)
+    spread = Spread(pooled, pooled_all, *sems)
     spread.start()
-    moves = [
-        Shift(cot_ref, cot_after.at[d - 1], sends.at[d - 1], recvs.at[d - 1], -d)
-        for d in range(1, hops + 1)
-    ]
-    for move in moves:
-        move.start()
-    spread.wait()
-    for move in moves:
-        move.wait()
+    spread.finish()
 
 
 def third_exchange(far, mixed_all, grad_all, mixed_in, grad_in, sends, recvs, local):
@@ -305,29 +402,48 @@
 
 
 def fine_forward(
-    pos, before, x_ref, after, w_ref, out_w,
-    q_all, k_all, v_all, unit_q, unit_k, scale_q, scale_k, tot_ref, att_ref, hidden_ref,
+    hops, x_ref, cot_ref, cg_ref, w_hbm, out_hbm,
+    q_all, k_all, v_all, unit_q, unit_k, scale_q, scale_k, tot_ref, att_ref, hidden_ref, cg_all,
+    after, cot_after,
+    before, w_ref, out_w, load, sends, recvs, *sems,
 ):
+    me, count, subs = place()
     rows = x_ref.shape[0]
-    margin = before.shape[0]
-    anchor = pos[0] * rows
+    margin = hops * rows
+    anchor = me * rows
+    loads = [
+        pltpu.make_async_copy(w_hbm, w_ref, load.at[0]),
+        pltpu.make_async_copy(out_hbm, out_w, load.at[1]),
+    ]
+    for one in loads:
+        one.start()
+    greet_all()
+    down = Halo(x_ref, before, sends.at[0], recvs.at[0], hops, 1)
+    up = Halo(x_ref, after, sends.at[1], recvs.at[1], hops, -1)
+    up_cot = Halo(cot_ref, cot_after, sends.at[2], recvs.at[2], hops, -1)
+    spread = Spread(cg_ref, cg_all, *sems)
+    down.start()
+    up.start()
+    up_cot.start()
+    spread.start()
     own = x_ref[...].astype(F32)
-    prev = before[...].astype(F32)
+    own_b = rms_rows(own)[0].astype(BF16)
+    loads[0].wait()
+    unit, factor = head_rms(dot(own_b, w_ref[0]))
+    q_all[...] = unit.astype(BF16)
+    unit_q[...] = unit
+    scale_q[...] = factor
+    unit, factor = head_rms(dot(own_b, w_ref[1]))
+    k_all[pl.ds(margin, rows), :] = unit.astype(BF16)
+    unit_k[...] = unit
+    scale_k[...] = factor
+    v_all[pl.ds(margin, rows), :] = dot(own_b, w_ref[2]).astype(BF16)
+    down.finish()
+    prev = before[...].reshape(margin, D).astype(F32)
     prev = jnp.where(anchor - margin + iota(prev.shape, 0) >= 0, prev, 0.0)
-    nxt = after[...].astype(F32)
-    nxt = jnp.where(anchor + rows + iota(nxt.shape, 0) < pos[1] * rows, nxt, 0.0)
-    own_b = rms_rows(own)[0].astype(BF16)
-    past_b = jnp.concatenate([rms_rows(prev)[0].astype(BF16), own_b])
-    next_b = jnp.concatenate([own_b, rms_rows(nxt)[0].astype(BF16)])
-    unit, factor = head_rms(dot(next_b, w_ref[0]))
-    q_all[...] = unit.astype(BF16)
-    unit_q[...] = unit[:rows]
-    scale_q[...] = factor[:rows]
-    unit, factor = head_rms(dot(past_b, w_ref[1]))
-    k_all[...] = unit.astype(BF16)
-    unit_k[...] = unit[margin:]
-    scale_k[...] = factor[margin:]
-    v_all[...] = dot(past_b, w_ref[2]).astype(BF16)
+    prev_b = rms_rows(prev)[0].astype(BF16)
+    k_all[pl.ds(0, margin), :] = head_rms(dot(prev_b, w_ref[1]))[0].astype(BF16)
+    v_all[pl.ds(0, margin), :] = dot(prev_b, w_ref[2]).astype(BF16)
     mask = window_mask(rows, margin + rows, anchor)
     mask = jnp.concatenate([mask.astype(F32)] * 2) > 0
     lane = iota((rows, 128), 1)
@@ -342,7 +458,14 @@
         totals = jnp.where(lane == 2 * p, t[:rows], totals)
         totals = jnp.where(lane == 2 * p + 1, t[rows:], totals)
     tot_ref[...] = totals
+    loads[1].wait()
     hidden_ref[...] = (own + dot(att_ref[...], out_w[...])).astype(BF16)
+    up.finish()
+    up_cot.finish()
+    spread.finish()
+    down.drain()
+    up.drain()
+    up_cot.drain()
 
 
 def coarse_level(pos, pooled_ref, cg_ref, w_ref, out_w, mixed_ref, grad_ref):
@@ -428,14 +551,18 @@
 
 
 def fine_backward(
-    pos, x_ref, w_ref, q_all, k_all, v_all, g_all, own_stats, after, tot_ref, delta_ref,
+    pos, x_ref, next_ref, w_ref, q_own, k_all, v_all, g_all, own_stats, after, tot_ref, delta_ref,
     unit_q, unit_k, scale_q, scale_k, hg_ref, grad_ref,
 ):
     rows = x_ref.shape[0]
     hops = after.shape[0]
     margin = k_all.shape[0] - rows
-    length = q_all.shape[0]
+    length = g_all.shape[0]
     anchor = pos[0] * rows
+    nxt = next_ref[...].astype(F32)
+    nxt = jnp.where(anchor + rows + iota(nxt.shape, 0) < pos[1] * rows, nxt, 0.0)
+    q_next = head_rms(dot(rms_rows(nxt)[0].astype(BF16), w_ref[0]))[0].astype(BF16)
+    q_all = jnp.concatenate([q_own[...], q_next])
     mask = window_mask(rows, margin + rows, anchor)
     mask = jnp.concatenate([mask.astype(F32)] * 2) > 0
     gap = iota((rows, length), 1) - iota((rows, length), 0)
@@ -446,7 +573,8 @@
     dq_p, dk_p, dv_p = [], [], []
     for p in range(HEADS // 2):
         cols = pl.ds(p * PAIR, PAIR)
-        kp, vp, qp, gp = k_all[:, cols], v_all[:, cols], q_all[:, cols], g_all[:, cols]
+        kp, vp, gp = k_all[:, cols], v_all[:, cols], g_all[:, cols]
+        qp = q_all[:, p * PAIR : (p + 1) * PAIR]
         s = dot_nt(both(qp[:rows]), kp) * SCALE
         e = jnp.where(mask, jnp.exp(s), 0.0)
         column = lambda m: jnp.concatenate([m[:, 2 * p : 2 * p + 1], m[:, 2 * p + 1 : 2 * p + 2]])
@@ -486,26 +614,23 @@
     fine_w = jnp.transpose(fine_qkv, (1, 0, 2))
     coarse_w = jnp.transpose(coarse_qkv, (1, 0, 2))
     coarse_grad = cotangent.astype(F32).reshape(outs, POOL, D).sum(axis=1).astype(BF16)
-    before, after, cg_all = comm(
-        functools.partial(first_exchange, hops),
-        (shape((hops, rows, D), BF16), shape((hops, rows, D), BF16), shape((count, outs, D), BF16)),
-        [dma((2 * hops,)), dma((2 * hops,)), dma((count,)), dma((count,)), dma],
-        0, [VMEM, VMEM], tokens, coarse_grad,
-    )
     length = (hops + 1) * rows
     flat = lambda a: a.reshape(-1, D)
-    q_all, k_all, v_all, unit_q, unit_k, scale_q, scale_k, totals, attended, hidden = local_call(
-        fine_forward,
-        [shape((length, D), BF16)] * 3 + [shape((rows, D), F32)] * 4
-        + [shape((rows, 128), F32)] + [shape((rows, D), BF16)] * 2,
-        pos, flat(before), tokens, flat(after), fine_w, fine_out,
-    )
-    pooled_all, cot_after = comm(
-        functools.partial(second_exchange, hops),
-        (shape((count, outs, D), BF16), shape((hops, rows, D), BF16)),
-        [pltpu.VMEM((POOL, D), BF16), pltpu.VMEM((outs, D), BF16), dma((hops + 1,)), dma((hops + 1,)),
-         dma((count,)), dma((count,)), dma],
-        1, [VMEM, VMEM], hidden, cotangent,
+    q_own, k_all, v_all, unit_q, unit_k, scale_q, scale_k, totals, attended, hidden, cg_all, after, cot_after = comm(
+        functools.partial(fine_forward, hops),
+        [shape((rows, D), BF16)] + [shape((length, D), BF16)] * 2 + [shape((rows, D), F32)] * 4
+        + [shape((rows, 128), F32)] + [shape((rows, D), BF16)] * 2
+        + [shape((count, outs, D), BF16)] + [shape((hops, rows, D), BF16)] * 2,
+        [pltpu.VMEM((hops, rows, D), BF16), pltpu.VMEM(fine_w.shape, BF16), pltpu.VMEM(fine_out.shape, BF16),
+         dma((2,)), dma((3, 2 * hops)), dma((3, hops))] + spread_sems(count, subs),
+        0, [VMEM] * 3 + [ANY] * 2, tokens, cotangent, coarse_grad, fine_w, fine_out,
+        out_specs=[VMEM] * 13,
+    )
+    pooled_all = comm(
+        second_exchange,
+        shape((count, outs, D), BF16),
+        [pltpu.VMEM((POOL, D), BF16), pltpu.VMEM((outs, D), BF16), dma, dma] + spread_sems(count, subs),
+        1, [VMEM], hidden, out_specs=VMEM,
     )
     pooled_all, cg_all = flat(pooled_all), flat(cg_all)
     mixed_all, grad_all = local_call(
@@ -535,7 +660,7 @@
     )
     grad_tokens = local_call(
         fine_backward, shape((rows, D), BF16),
-        pos, tokens, fine_w, q_all, k_all, v_all, g_all, stats, stats_after, totals, delta,
+        pos, tokens, flat(after), fine_w, q_own, k_all, v_all, g_all, stats, stats_after, totals, delta,
         unit_q, unit_k, scale_q, scale_k, hidden_grad,
     )
     return (output, grad_tokens)

time: 155 us -> 133 us (0.86)
  Pallas kernels: 150 us -> 126 us
    pallas_call x4 -> x3, Pallas kernels: 49.7 us -> 35.4 us  [local_call(): pl.pallas_call(body, out_shape=outs, in_specs=[SMEM] + [VMEM] * (len(args...]
    pallas_call x4, Pallas kernels: 100 us -> 90.7 us  [comm(): pl.pallas_call(body, out_shape=outs, in_specs=specs, out_specs=jax.tree.m...]
where the time goes in v2:
time: 133 us; the launch traced here: 131 us
  Pallas kernels  126 us (95%)
  other arithmetic  2.3 us (2%)
  local copies, waits for them, and re-layouts  1.66 us (1%)
    pallas_call x4, Pallas kernels, comm(): pl.pallas_call(body, out_shape=outs, in_specs=specs, out_specs=jax.tree.m...  90.7 us
    pallas_call x3, Pallas kernels, local_call(): pl.pallas_call(body, out_shape=outs, in_specs=[SMEM] + [VMEM] * (len(args...  35.4 us

profile of v2, /device:TPU:5, one launch (start us, length us, event | category | flops | bytes accessed | tf_op | source)
XLA Modules:
  0.0 130.8 jit_solution(14880643580479796131)
XLA Ops:
  0.6 0.6 pad_add_fusion.pos
  1.3 1.7 %bitcast_reduce_fusion.cg_ref = bf16[8,1024]{1,0:T(8,128)(2,1)} fusion(bf16[128,1024]{1,0:T(8,128)(2,1)} %cot_ref.3), kind=kLoop, calls=%fused_computation.2 | loop fusion | flops 122880 | bytes 278528 | tf_op jit(solution)/shard_map/reduce_sum | solution.py:616
  2.9 61.0 %shard_map.77 = (bf16[128,1024]{1,0:T(8,128)(2,1)}, bf16[640,1024]{1,0:T(8,128)(2,1)}, bf16[640,1024]{1,0:T(8,128)(2,1)}, f32[128,1024]{1,0:T(8,128)}, f32[128,1...) custom-call(bf16[128,1024]{1,0:T(8,128)(2,1)} %x_ref.3, ...), custom_call_target="tpu_custom_call" | custom-call | tf_op jit(solution)/shard_map/pallas_call | solution.py:299
  63.9 16.8 %shard_map.78 = bf16[32,8,1024]{2,1,0:T(8,128)(2,1)} custom-call(bf16[128,1024]{1,0:T(8,128)(2,1)} %get-tuple-element.24.hidden_ref), custom_call_target="tpu_custom_call" | custom-call | tf_op jit(solution)/shard_map/pallas_call | solution.py:299
  80.7 1.7 %pad_dynamic-slice_fusion = (bf16[48,1024]{1,0:T(8,128)(2,1)}, bf16[48,1024]{1,0:T(8,128)(2,1)}) fusion(s32[]{:T(128)S(6)} %select_n.4, bf16[256,1024]{1,0:T(8,128)(2,1)} %bitcast.14, bf16[256,1024]{1,0:T(8,128)(2,1)} %bitcast.11), kind=kLoop, calls=%fused_computation | loop fusion | bytes 1245188 | tf_op jit(solution)/shard_map/dynamic_slice | solution.py:647
  82.4 10.5 %shard_map.79 = (bf16[256,1024]{1,0:T(8,128)(2,1)}, bf16[304,1024]{1,0:T(8,128)(2,1)}) custom-call(s32[2]{0:T(128)} %pad_add_fusion.pos, bf16[256,1024]{1,0:T(8,128)(2,1)} %bitcast.12, bf16[256,1024]{1,0:T(8,128)(2,1)} %bitcast.15, bf16[3,1024,512]{2,1,0:T(8,128)(2,1)} %bitcast.13, bf16[512,1024]{1,0:T(8,128)(2,1)} %out_w.2), custom_call_target="tpu_custom_call" | custom-call | tf_op jit(solution)/shard_map/pallas_call | solution.py:312
  92.9 6.0 %shard_map.80 = (bf16[2,8,1024]{2,1,0:T(8,128)(2,1)}, bf16[2,48,1024]{2,1,0:T(8,128)(2,1)}) custom-call(bf16[256,1024]{1,0:T(8,128)(2,1)} %get-tuple-element.26.mixed_all, bf16[304,1024]{1,0:T(8,128)(2,1)} %get-tuple-element.27.grad_all), custom_call_target="tpu_custom_call" | custom-call | tf_op jit(solution)/shard_map/pallas_call | solution.py:299
  98.9 6.0 %shard_map.81 = (bf16[128,1024]{1,0:T(8,128)(2,1)}, f32[128,1024]{1,0:T(8,128)}, bf16[640,1024]{1,0:T(8,128)(2,1)}, f32[128,128]{1,0:T(8,128)}, f32[32,128]{1,0:T(8,128)}) custom-call(s32[2]{0:T(128)} %pad_add_fusion.pos, bf16[128,1024]{1,0:T(8,128)(2,1)} %get-tuple-element.24.hidden_ref, bf16[2,8,1024]{2,1,0:T(8,128)(2,1)} %get-tuple-element.28.mixed_in, ...), custom_call_target="tpu_custom_call" | custom-call | tf_op jit(solution)/shard_map/pallas_call | solution.py:312
  104.9 6.9 %shard_map.82.after = f32[4,32,128]{2,1,0:T(8,128)} custom-call(f32[32,128]{1,0:T(8,128)} %get-tuple-element.39.stats_ref.own_stats), custom_call_target="tpu_custom_call" | custom-call | tf_op jit(solution)/shard_map/pallas_call | solution.py:299
  111.8 18.9 %shard_map.83 = bf16[128,1024]{1,0:T(8,128)(2,1)} custom-call(s32[2]{0:T(128)} %pad_add_fusion.pos, bf16[128,1024]{1,0:T(8,128)(2,1)} %x_ref.3, bf16[512,1024]{1,0:T(8,128)(2,1)} %bitcast.16, bf16[3,1024,1024]{2,1,0:T(8,128)(2,1)} %bitcast.10, bf16[128,1024]{1,0:T(8,128)(2,1)} %get-tuple-element.35.q_own, bf16[640,1024]{1,0:T(8,128)(2,1)} %get-tuple-element.36.k_all, ...), custom_call_target="tpu_custom_call" | custom-call | tf_op jit(solution)/shard_map/pallas_call | solution.py:312

commit v3 on v2

--- a/solution.py
+++ b/solution.py
@@ -423,8 +423,6 @@
     up_cot = Halo(cot_ref, cot_after, sends.at[2], recvs.at[2], hops, -1)
     spread = Spread(cg_ref, cg_all, *sems)
     down.start()
-    up.start()
-    up_cot.start()
     spread.start()
     own = x_ref[...].astype(F32)
     own_b = rms_rows(own)[0].astype(BF16)
@@ -439,6 +437,8 @@
     scale_k[...] = factor
     v_all[pl.ds(margin, rows), :] = dot(own_b, w_ref[2]).astype(BF16)
     down.finish()
+    up.start()
+    up_cot.start()
     prev = before[...].reshape(margin, D).astype(F32)
     prev = jnp.where(anchor - margin + iota(prev.shape, 0) >= 0, prev, 0.0)
     prev_b = rms_rows(prev)[0].astype(BF16)

time: 133 us -> 132 us (level)
  no operation moved by 1% of the time
where the time goes in v3:
time: 132 us; the launch traced here: 130 us
  Pallas kernels  126 us (95%)
  other arithmetic  2.3 us (2%)
  local copies, waits for them, and re-layouts  1.66 us (1%)
    pallas_call x4, Pallas kernels, comm(): pl.pallas_call(body, out_shape=outs, in_specs=specs, out_specs=jax.tree.m...  90.1 us
    pallas_call x3, Pallas kernels, local_call(): pl.pallas_call(body, out_shape=outs, in_specs=[SMEM] + [VMEM] * (len(args...  35.4 us

profile of v3, /device:TPU:5, one launch (start us, length us, event | category | flops | bytes accessed | tf_op | source)
XLA Modules:
  0.0 130.1 jit_solution(13834113394579032714)
XLA Ops:
  0.6 0.6 pad_add_fusion.pos
  1.3 1.7 %bitcast_reduce_fusion.cg_ref = bf16[8,1024]{1,0:T(8,128)(2,1)} fusion(bf16[128,1024]{1,0:T(8,128)(2,1)} %cot_ref.3), kind=kLoop, calls=%fused_computation.2 | loop fusion | flops 122880 | bytes 278528 | tf_op jit(solution)/shard_map/reduce_sum | solution.py:616
  2.9 57.7 %shard_map.77 = (bf16[128,1024]{1,0:T(8,128)(2,1)}, bf16[640,1024]{1,0:T(8,128)(2,1)}, bf16[640,1024]{1,0:T(8,128)(2,1)}, f32[128,1024]{1,0:T(8,128)}, f32[128,1...) custom-call(bf16[128,1024]{1,0:T(8,128)(2,1)} %x_ref.3, ...), custom_call_target="tpu_custom_call" | custom-call | tf_op jit(solution)/shard_map/pallas_call | solution.py:299
  60.7 20.2 %shard_map.78 = bf16[32,8,1024]{2,1,0:T(8,128)(2,1)} custom-call(bf16[128,1024]{1,0:T(8,128)(2,1)} %get-tuple-element.24.hidden_ref), custom_call_target="tpu_custom_call" | custom-call | tf_op jit(solution)/shard_map/pallas_call | solution.py:299
  80.9 1.7 %pad_dynamic-slice_fusion = (bf16[48,1024]{1,0:T(8,128)(2,1)}, bf16[48,1024]{1,0:T(8,128)(2,1)}) fusion(s32[]{:T(128)S(6)} %select_n.4, bf16[256,1024]{1,0:T(8,128)(2,1)} %bitcast.14, bf16[256,1024]{1,0:T(8,128)(2,1)} %bitcast.11), kind=kLoop, calls=%fused_computation | loop fusion | bytes 1245188 | tf_op jit(solution)/shard_map/dynamic_slice | solution.py:647
  82.5 10.5 %shard_map.79 = (bf16[256,1024]{1,0:T(8,128)(2,1)}, bf16[304,1024]{1,0:T(8,128)(2,1)}) custom-call(s32[2]{0:T(128)} %pad_add_fusion.pos, bf16[256,1024]{1,0:T(8,128)(2,1)} %bitcast.12, bf16[256,1024]{1,0:T(8,128)(2,1)} %bitcast.15, bf16[3,1024,512]{2,1,0:T(8,128)(2,1)} %bitcast.13, bf16[512,1024]{1,0:T(8,128)(2,1)} %out_w.2), custom_call_target="tpu_custom_call" | custom-call | tf_op jit(solution)/shard_map/pallas_call | solution.py:312
  93.0 6.0 %shard_map.80 = (bf16[2,8,1024]{2,1,0:T(8,128)(2,1)}, bf16[2,48,1024]{2,1,0:T(8,128)(2,1)}) custom-call(bf16[256,1024]{1,0:T(8,128)(2,1)} %get-tuple-element.26.mixed_all, bf16[304,1024]{1,0:T(8,128)(2,1)} %get-tuple-element.27.grad_all), custom_call_target="tpu_custom_call" | custom-call | tf_op jit(solution)/shard_map/pallas_call | solution.py:299
  99.1 6.0 %shard_map.81 = (bf16[128,1024]{1,0:T(8,128)(2,1)}, f32[128,1024]{1,0:T(8,128)}, bf16[640,1024]{1,0:T(8,128)(2,1)}, f32[128,128]{1,0:T(8,128)}, f32[32,128]{1,0:T(8,128)}) custom-call(s32[2]{0:T(128)} %pad_add_fusion.pos, bf16[128,1024]{1,0:T(8,128)(2,1)} %get-tuple-element.24.hidden_ref, bf16[2,8,1024]{2,1,0:T(8,128)(2,1)} %get-tuple-element.28.mixed_in, ...), custom_call_target="tpu_custom_call" | custom-call | tf_op jit(solution)/shard_map/pallas_call | solution.py:312
  105.1 6.1 %shard_map.82.after = f32[4,32,128]{2,1,0:T(8,128)} custom-call(f32[32,128]{1,0:T(8,128)} %get-tuple-element.39.stats_ref.own_stats), custom_call_target="tpu_custom_call" | custom-call | tf_op jit(solution)/shard_map/pallas_call | solution.py:299
  111.2 18.9 %shard_map.83 = bf16[128,1024]{1,0:T(8,128)(2,1)} custom-call(s32[2]{0:T(128)} %pad_add_fusion.pos, bf16[128,1024]{1,0:T(8,128)(2,1)} %x_ref.3, bf16[512,1024]{1,0:T(8,128)(2,1)} %bitcast.16, bf16[3,1024,1024]{2,1,0:T(8,128)(2,1)} %bitcast.10, bf16[128,1024]{1,0:T(8,128)(2,1)} %get-tuple-element.35.q_own, bf16[640,1024]{1,0:T(8,128)(2,1)} %get-tuple-element.36.k_all, ...), custom_call_target="tpu_custom_call" | custom-call | tf_op jit(solution)/shard_map/pallas_call | solution.py:312
